TPU v7x, 128 devices: a whole 4x4x4 slice. The times are simulated.
128 devices in a mesh: node: 32 (over x, z, core), feat: 4 (over y).
Axes of the slice: x: 4, y: 4, z: 4, core: 2. Of those that a mesh axis runs over, the one named last changes fastest.
Arguments:
- features: bfloat16 [100, 32768], P('feat', 'node'), may hold values from -6 to 6
- edges_one: int32 [1024, 32768], P(None, 'node'), may hold values from 0 to 1, as said below
- w1_self: bfloat16 [100, 256], P('feat'), may hold values from -0.625 to 0.625
- w1_nbr: bfloat16 [100, 256], P('feat'), may hold values from -1.25 to 1.25
- need_blocks: int32 [32, 4], P('node'), may hold values from 0 to 31, as said below
- live_slots: int32 [32, 4], P('node'), may hold values from 0 to 1, as said below
- edges_two: int32 [4096, 32768], P(None, 'node'), may hold values from 0 to 1, as said below
- w2_self: bfloat16 [256, 47], P('feat'), may hold values from -0.375 to 0.375
- w2_nbr: bfloat16 [256, 47], P('feat'), may hold values from -0.5 to 0.5
- labels: int32 [32768], P('node'), may hold values from 0 to 46
Outputs:
- node_loss: float32 [32768], P('node')
- mean_loss: float32 [], replicated
Inputs may be any that keep to these rules, and one draw needn't show every extreme that they name: `need_blocks`: row b holds 4 different blocks; its first entry is b, its second is b plus half the number of blocks, its third is b minus 1, and its entry k is b plus an offset that depends on k alone, modulo the number of blocks. `live_slots`: the first three entries of each row are 1. `edges_one`: each column has exactly 25 ones. `edges_two`: each column t has exactly 10 ones, all in rows of slots that live_slots marks as used for t's block.
All inputs are finite; a program needn't handle non-finite values.
Results may differ from a plain program's by a relative error of at most 0.00065.
Values may be sent and summed in bfloat16 or wider, within the bound.
No kernel may reach another device: no remote copies, remote signals or barrier semaphores. Data moves between devices by JAX's collectives and lax.ppermute only.
A program may use at most 128 MiB of HBM per device.

v0:
```python
import functools

import jax
import jax.numpy as jnp
from jax import lax
from jax.experimental import pallas as pl
from jax.experimental.pallas import tpu as pltpu
from jax.sharding import PartitionSpec as P

FAN1 = 25
FAN2 = 10
LANES = 128
WORDS = 32
MIB = 1 << 20

VMEM = pl.BlockSpec(memory_space=pltpu.VMEM)
HBM = pl.BlockSpec(memory_space=pltpu.HBM)
SMEM = pl.BlockSpec(memory_space=pltpu.SMEM)


def in_hbm(value):
    return pltpu.with_memory_space_constraint(value, pltpu.HBM)


def from_ahead(value, axis, steps):
    count = lax.axis_size(axis)
    pairs = [(source, (source - steps) % count) for source in range(count)]
    return lax.ppermute(value, axis, pairs)


def pack_kernel(nodes, *refs):
    sources, (out_ref, off_ref), held, (scr, cat, sems) = refs[:6], refs[6:8], refs[8:14], refs[14:]
    copies = [
        pltpu.make_async_copy(source, place, sems.at[index])
        for index, (source, place) in enumerate(zip(sources, held))
    ]
    for copy in copies:
        copy.start()
    x_ref, ws_ref, wn_ref, us_ref, un_ref, need_ref = held
    rows, cols = x_ref.shape
    hid = ws_ref.shape[1]
    classes, depth = us_ref.shape
    spare = out_ref.shape[0] - rows
    bands = pl.cdiv(classes, spare)
    scr[rows:, :] = jnp.zeros((spare, scr.shape[1]), jnp.float32)
    for copy in copies:
        copy.wait()
    scr[:rows, :cols] = x_ref[...].astype(jnp.float32)
    scr[:rows, cols : cols + hid] = ws_ref[...].astype(jnp.float32)
    scr[:rows, cols + hid :] = wn_ref[...].astype(jnp.float32)
    cat[:classes, :depth] = us_ref[...].astype(jnp.float32)
    cat[:classes, depth:] = un_ref[...].astype(jnp.float32)
    for band in range(bands):
        first = band * spare
        count = min(spare, classes - first)
        scr[rows : rows + count, band * LANES : (band + 1) * LANES] = cat[first : first + count, :]
    out_ref[...] = scr[...].astype(jnp.bfloat16)
    offset = lax.rem(need_ref[0, 3] - lax.axis_index("node") + nodes, nodes)
    off_ref[0] = offset - 1 - (offset > nodes // 2).astype(jnp.int32)


def packed_bits(piece, first_bit):
    words = None
    for group in range(piece.shape[0] // WORDS):
        bits = piece[group * WORDS : (group + 1) * WORDS, :] << (first_bit + group)
        words = bits if words is None else words | bits
    return words


def load_kernel(e1_ref, e2_ref, after_ref, e1_out, bits_ref, held, sems):
    pieces = held.shape[0]
    rows = held.shape[1]
    base = e1_ref.shape[0]
    copies = [
        pltpu.make_async_copy(
            e2_ref.at[pl.ds(base + index * rows, rows)], held.at[index], sems.at[index]
        )
        for index in range(pieces)
    ]
    copies.append(pltpu.make_async_copy(e1_ref, e1_out, sems.at[pieces]))
    for copy in copies:
        copy.start()
    words = jnp.zeros(bits_ref.shape, jnp.int32)
    for index in range(pieces):
        copies[index].wait()
        words = words | packed_bits(held.at[index], index * (rows // WORDS))
    bits_ref[...] = words
    copies[pieces].wait()


def stream_kernel(z_ref, self_ref, e2_ref, total_ref, bits_ref, held, acc, sems):
    rows = held.shape[1]
    cols = z_ref.shape[1]
    pieces = cols // rows
    sources = [slot * pieces + index for slot in (0, 2, 3) for index in range(pieces)]
    copies = [
        pltpu.make_async_copy(e2_ref.at[pl.ds(source * rows, rows)], held.at[index], sems.at[index])
        for index, source in enumerate(sources)
    ]
    for copy in copies:
        copy.start()
    acc[...] = jnp.zeros_like(acc)

    def arrived(index):
        pltpu.make_async_copy(e2_ref.at[pl.ds(0, rows)], held.at[index], sems.at[index]).wait()
        return held.at[index]

    @pl.loop(0, pieces)
    def _(index):
        adjacency = arrived(index)[...].astype(jnp.float32).astype(jnp.bfloat16)
        own = z_ref[:, pl.ds(pl.multiple_of(index * rows, rows), rows)]
        acc[...] += jnp.dot(own, adjacency, preferred_element_type=jnp.float32)

    total_ref[...] = self_ref[...] + acc[...] / FAN2
    bits_ref[...] = jnp.zeros_like(bits_ref)

    @pl.loop(pieces, 3 * pieces)
    def _(index):
        slot = index // pieces - 1
        piece = arrived(index)
        bits_ref[slot] = bits_ref[slot] | packed_bits(piece, (index % pieces) * (rows // WORDS))


def first_kernel(
    rows, hid, classes, p0_ref, p1_ref, p2_ref, p3_ref, e_ref, self_ref, z_ref, blocks, w2, w1
):
    me = lax.axis_index("feat")
    feats, height, width = blocks.shape
    cols = width - 2 * hid
    spare = height - rows
    for step, ref in enumerate((p0_ref, p1_ref, p2_ref, p3_ref)):
        blocks[lax.rem(me + step, feats)] = ref[...]
    bands = pl.cdiv(classes, spare)
    for f in range(feats):
        for band in range(bands):
            count = min(spare, classes - band * spare)
            tail = blocks[f, :, band * LANES : (band + 1) * LANES].astype(jnp.float32)
            w2[f, band * spare : band * spare + count, :] = tail[rows : rows + count]
        w2[f, classes:, :] = jnp.zeros((w2.shape[1] - classes, LANES), jnp.float32)
    half = LANES // 2
    low = lax.broadcasted_iota(jnp.int32, (w2.shape[1], LANES), 1) < half
    selfs, nbrs = [], []
    for f in range(0, feats, 2):
        a, b = w2[f], w2[f + 1]
        selfs.append(jnp.where(low, a, pltpu.roll(b, half, 1)))
        nbrs.append(jnp.where(low, pltpu.roll(a, half, 1), b))
    project = jnp.concatenate(
        [jnp.concatenate(selfs, axis=1), jnp.concatenate(nbrs, axis=1)], axis=0
    ).astype(jnp.bfloat16)
    inputs = blocks[:, :, :cols].reshape(feats * height, cols)
    w1[: feats * height, :] = blocks[:, :, cols : cols + hid].reshape(feats * height, hid)
    w1[feats * height :, :] = blocks[:, :, cols + hid :].reshape(feats * height, hid)
    weights = w1[...]
    padded = w2.shape[1]
    chunk = 256
    for first in range(0, cols, chunk):
        part = slice(first, first + chunk)
        adjacency = e_ref[:, part].astype(jnp.float32).astype(jnp.bfloat16)
        nbr = jnp.dot(inputs, adjacency, preferred_element_type=jnp.float32) / FAN1
        stacked = jnp.concatenate([inputs[:, part], nbr.astype(jnp.bfloat16)], axis=0)
        before = lax.dot_general(
            weights, stacked, (((0,), (0,)), ((), ())), preferred_element_type=jnp.float32
        )
        hidden = jnp.maximum(before, 0.0).astype(jnp.bfloat16)
        both = jnp.dot(project, hidden, preferred_element_type=jnp.float32)
        self_ref[:, part] = both[:padded]
        z_ref[:, part] = both[padded:].astype(jnp.bfloat16)


def second_kernel(
    classes, z1_ref, z2_ref, z3_ref, total_ref, live_ref, b1_ref, b23_ref, label_ref, loss_ref, sum_ref, zs
):
    padded, cols = total_ref.shape
    chunk = 256
    group = lax.broadcasted_iota(jnp.int32, (1, cols), 1) // WORDS
    scale = jnp.ones((1, cols), jnp.float32)
    for bit in range(5):
        scale = scale * jnp.where((group >> bit) % 2 == 1, 2.0 ** -(1 << bit), 1.0)
    scale = jnp.where(group == 31, -scale, scale)
    for slot, ref in enumerate((z1_ref, z2_ref, z3_ref)):
        used = jnp.where(live_ref[0, slot + 1] == 1, scale, 0.0)
        zs[:, slot * cols : (slot + 1) * cols] = (ref[...].astype(jnp.float32) * used).astype(
            jnp.bfloat16
        )
    class_ids = lax.broadcasted_iota(jnp.int32, (padded, chunk), 0)
    summed = jnp.zeros((1, chunk), jnp.float32)
    for first in range(0, cols, chunk):
        part = slice(first, first + chunk)
        term = jnp.zeros((padded, chunk), jnp.float32)
        for slot, words in enumerate((b1_ref[:, part], b23_ref[0, :, part], b23_ref[1, :, part])):
            planes = []
            for bit in range(32):
                mask = (1 << bit) if bit < 31 else -(1 << 31)
                planes.append((words & jnp.int32(mask)).astype(jnp.float32).astype(jnp.bfloat16))
            adjacency = jnp.concatenate(planes, axis=0)
            term = term + jnp.dot(
                zs[:, slot * cols : (slot + 1) * cols], adjacency, preferred_element_type=jnp.float32
            )
        logits = total_ref[:, part] + term / FAN2
        powers = jnp.where(class_ids < classes, jnp.exp(logits), 0.0)
        picked = jnp.where(class_ids == label_ref[:, part], logits, 0.0)
        loss = jnp.log(jnp.sum(powers, 0, keepdims=True)) - jnp.sum(picked, 0, keepdims=True)
        loss_ref[:, part] = loss
        summed = summed + loss
    mean = jnp.sum(summed, keepdims=True) / (cols * sum_ref.shape[0])
    sum_ref[...] = jnp.broadcast_to(mean.reshape(1, 1, 1), sum_ref.shape)


def local(
    features,
    edges_one,
    w1_self,
    w1_nbr,
    need_blocks,
    live_slots,
    edges_two,
    w2_self,
    w2_nbr,
    labels,
):
    rows, block_len = features.shape
    hid = w1_self.shape[1]
    depth, classes = w2_self.shape
    nodes = lax.axis_size("node")
    feats = lax.axis_size("feat")
    height = pl.cdiv(rows, 8) * 8
    width = block_len + 2 * hid
    padded = pl.cdiv(classes, 16) * 16

    packed, number = pl.pallas_call(
        functools.partial(pack_kernel, nodes),
        out_shape=(
            jax.ShapeDtypeStruct((height, width), jnp.bfloat16),
            jax.ShapeDtypeStruct((1,), jnp.int32),
        ),
        in_specs=[HBM] * 6,
        out_specs=(VMEM, SMEM),
        scratch_shapes=[
            pltpu.VMEM((rows, block_len), jnp.bfloat16),
            pltpu.VMEM((rows, hid), jnp.bfloat16),
            pltpu.VMEM((rows, hid), jnp.bfloat16),
            pltpu.VMEM((classes, depth), jnp.bfloat16),
            pltpu.VMEM((classes, depth), jnp.bfloat16),
            pltpu.SMEM(need_blocks.shape, jnp.int32),
            pltpu.VMEM((height, width), jnp.float32),
            pltpu.VMEM((padded, 2 * depth), jnp.float32),
            pltpu.SemaphoreType.DMA((6,)),
        ],
        compiler_params=pltpu.CompilerParams(vmem_limit_bytes=4 * MIB),
        cost_estimate=pl.CostEstimate(flops=2 * MIB, bytes_accessed=MIB // 4, transcendentals=0),
        name="pack",
    )(*map(in_hbm, (features, w1_self, w1_nbr, w2_self.T, w2_nbr.T, need_blocks)))

    blocks = [packed] + [from_ahead(packed, "feat", step) for step in range(1, feats)]
    words = block_len // 32
    edges_one, bits_one = pl.pallas_call(
        load_kernel,
        out_shape=(
            jax.ShapeDtypeStruct(edges_one.shape, jnp.int32),
            jax.ShapeDtypeStruct((words, block_len), jnp.int32),
        ),
        in_specs=[HBM, HBM, VMEM],
        out_specs=(VMEM, VMEM),
        scratch_shapes=[
            pltpu.VMEM((4, block_len // 4, block_len), jnp.int32),
            pltpu.SemaphoreType.DMA((5,)),
        ],
        compiler_params=pltpu.CompilerParams(vmem_limit_bytes=8 * MIB),
        cost_estimate=pl.CostEstimate(flops=100 * MIB, bytes_accessed=8 * MIB, transcendentals=0),
        name="load",
    )(in_hbm(edges_one), in_hbm(edges_two), packed)

    self_term, mine = pl.pallas_call(
        functools.partial(first_kernel, rows, hid, classes),
        out_shape=(
            jax.ShapeDtypeStruct((padded, block_len), jnp.float32),
            pltpu.VMEM((padded, block_len), jnp.bfloat16),
        ),
        in_specs=[VMEM] * 5,
        out_specs=(VMEM, VMEM),
        scratch_shapes=[
            pltpu.VMEM((feats, height, width), jnp.bfloat16),
            pltpu.VMEM((feats, padded, LANES), jnp.float32),
            pltpu.VMEM((2 * feats * height, hid), jnp.bfloat16),
        ],
        compiler_params=pltpu.CompilerParams(vmem_limit_bytes=16 * MIB),
        cost_estimate=pl.CostEstimate(
            flops=2 * 128 * block_len * block_len, bytes_accessed=4 * MIB, transcendentals=0
        ),
        name="first",
    )(*blocks, edges_one)

    half = from_ahead(mine, "node", nodes // 2)
    behind = from_ahead(mine, "node", nodes - 1)

    def with_offset(step, own, self_term, edges_two):
        fourth = from_ahead(own, "node", step)
        total, bits_rest = pl.pallas_call(
            stream_kernel,
            out_shape=(
                jax.ShapeDtypeStruct((padded, block_len), jnp.float32),
                jax.ShapeDtypeStruct((2, words, block_len), jnp.int32),
            ),
            in_specs=[VMEM, VMEM, HBM],
            out_specs=(VMEM, VMEM),
            scratch_shapes=[
                pltpu.VMEM((12, block_len // 4, block_len), jnp.int32),
                pltpu.VMEM((padded, block_len), jnp.float32),
                pltpu.SemaphoreType.DMA((12,)),
            ],
            compiler_params=pltpu.CompilerParams(vmem_limit_bytes=24 * MIB),
            cost_estimate=pl.CostEstimate(
                flops=100 * MIB, bytes_accessed=12 * MIB, transcendentals=0
            ),
            name="stream",
        )(own, self_term, in_hbm(edges_two))
        return fourth, total, bits_rest

    taken = (0, nodes // 2, nodes - 1)
    steps = [step for step in range(nodes) if step not in taken]
    fourth, total, bits_rest = lax.switch(
        number[0],
        [functools.partial(with_offset, step) for step in steps],
        mine,
        self_term,
        edges_two,
    )

    loss, sums = pl.pallas_call(
        functools.partial(second_kernel, classes),
        out_shape=(
            jax.ShapeDtypeStruct((1, block_len), jnp.float32),
            jax.ShapeDtypeStruct((nodes, 1, LANES), jnp.float32),
        ),
        in_specs=[VMEM] * 4 + [SMEM] + [VMEM] * 3,
        out_specs=(VMEM, VMEM),
        scratch_shapes=[pltpu.VMEM((padded, 3 * block_len), jnp.bfloat16)],
        compiler_params=pltpu.CompilerParams(vmem_limit_bytes=16 * MIB),
        cost_estimate=pl.CostEstimate(
            flops=2 * 64 * 3 * block_len * block_len,
            bytes_accessed=2 * MIB,
            transcendentals=padded * block_len,
        ),
        name="second",
    )(half, behind, fourth, total, live_slots, bits_one, bits_rest, labels[None, :])

    everyone = lax.all_to_all(sums, "node", 0, 0, tiled=True)
    mean_loss = jnp.sum(everyone[:, 0, 0])
    return (loss[0], mean_loss)


def solution(mesh):
    return jax.shard_map(
        local,
        mesh=mesh,
        in_specs=(
            P("feat", "node"),
            P(None, "node"),
            P("feat", None),
            P("feat", None),
            P("node", None),
            P("node", None),
            P(None, "node"),
            P("feat", None),
            P("feat", None),
            P("node"),
        ),
        out_specs=(P("node"), P()),
        check_vma=False,
    )
```

profile of v0, /device:TPU:1, one launch (start us, length us, event | category | flops | bytes accessed | tf_op | source)
XLA Modules:
  0.0 45.5 jit_solution(12067707457775171148)
XLA Ops:
  0.6 1.4 %pack.1 = (bf16[32,1536]{1,0:T(8,128)(2,1)S(1)}, s32[1]{0:T(128)}) custom-call(bf16[25,1024]{1,0:T(8,128)(2,1)} %refs_0_.1, bf16[25,256]{1,0:T(8,128)(2,1)} %refs_1_.1, bf16[25,256]{1,0:T(8,128)(2,1)} %refs_2_.1, bf16[47,64]{1,0:T(8,128)(2,1)} %bitcast.6, bf16[47,64]{1,0:T(8,128)(2,1)} %bitcast.7, s32[1,4]{1,0:T(1,128)} %refs_5_.1), custom_call_target="tpu_custom_call" | custom-call | flops 2097152 | bytes 262144 | tf_op jit(solution)/shard_map/pack/pallas_call | solution.py:230
  2.1 2.2 %collective-permute-start.31 = (bf16[32,1536]{1,0:T(8,128)(2,1)S(1)}, bf16[32,1536]{1,0:T(8,128)(2,1)S(1)}, u32[]{:S(2)}, u32[]{:S(2)}) collective-permute-start(bf16[32,1536]{1,0:T(8,128)(2,1)S(1)} %get-tuple-element.332.after_ref.p0_ref), channel_id=1, source_target_pairs={{0,1},{1,2},{2,3},{3,0},{4,5},{5,6},{6,7},{7,4},{8,9},{9,10},{10,1... | collective-permute-start | bytes 294920 | tf_op jit(solution)/shard_map/ppermute | solution.py:28
  4.3 2.6 %collective-permute-start.30 = (bf16[32,1536]{1,0:T(8,128)(2,1)S(1)}, bf16[32,1536]{1,0:T(8,128)(2,1)S(1)}, u32[]{:S(2)}, u32[]{:S(2)}) collective-permute-start(bf16[32,1536]{1,0:T(8,128)(2,1)S(1)} %get-tuple-element.332.after_ref.p0_ref), channel_id=1, source_target_pairs={{0,2},{1,3},{2,0},{3,1},{4,6},{5,7},{6,4},{7,5},{8,10},{9,11},{10,... | collective-permute-start | bytes 294920 | tf_op jit(solution)/shard_map/ppermute | solution.py:28
  6.9 1.1 %collective-permute-start.29 = (bf16[32,1536]{1,0:T(8,128)(2,1)S(1)}, bf16[32,1536]{1,0:T(8,128)(2,1)S(1)}, u32[]{:S(2)}, u32[]{:S(2)}) collective-permute-start(bf16[32,1536]{1,0:T(8,128)(2,1)S(1)} %get-tuple-element.332.after_ref.p0_ref), channel_id=1, source_target_pairs={{0,3},{1,0},{2,1},{3,2},{4,7},{5,4},{6,5},{7,6},{8,11},{9,8},{10,9... | collective-permute-start | bytes 294920 | tf_op jit(solution)/shard_map/ppermute | solution.py:28
  8.0 3.5 %load.1 = (s32[1024,1024]{1,0:T(8,128)S(1)}, s32[32,1024]{1,0:T(8,128)S(1)}) custom-call(s32[1024,1024]{1,0:T(8,128)} %e1_ref.1, s32[4096,1024]{1,0:T(8,128)} %e2_ref.1, bf16[32,1536]{1,0:T(8,128)(2,1)S(1)} %get-tuple-element.332.after_ref.p0_ref), custom_call_target="tpu_custom_call" | custom-call | flops 104857600 | bytes 8388608 | tf_op jit(solution)/shard_map/load/pallas_call | solution.py:256
  11.5 0.0 collective-permute-done.31.p3_ref
  11.5 0.0 collective-permute-done.30.p2_ref
  11.5 0.0 collective-permute-done.29.p1_ref
  11.5 2.7 %first.1 = (f32[48,1024]{1,0:T(8,128)S(1)}, bf16[48,1024]{1,0:T(8,128)(2,1)}) custom-call(bf16[32,1536]{1,0:T(8,128)(2,1)S(1)} %get-tuple-element.332.after_ref.p0_ref, bf16[32,1536]{1,0:T(8,128)(2,1)S(1)} %collective-permute-done.29.p1_ref, bf16[32,1536]{1,0:T(8,128)(2,1)S(1)} %collective-permute-done.30.p2_ref, ...), custom_call_target="tpu_custom_call" | custom-call | flops 268435456 | bytes 4194304 | tf_op jit(solution)/shard_map/first/pallas_call | solution.py:273
  14.2 3.0 %collective-permute-start.33 = (bf16[48,1024]{1,0:T(8,128)(2,1)}, bf16[48,1024]{1,0:T(8,128)(2,1)S(1)}, u32[]{:S(2)}, u32[]{:S(2)}) collective-permute-start(bf16[48,1024]{1,0:T(8,128)(2,1)} %get-tuple-element.334), channel_id=1, source_target_pairs={{0,4},{4,8},{8,12},{12,16},{16,20},{20,24},{24,28},{28,32},{32,36}... | collective-permute-start | bytes 294920 | tf_op jit(solution)/shard_map/ppermute | solution.py:28
  17.2 2.7 %collective-permute-start.32 = (bf16[48,1024]{1,0:T(8,128)(2,1)}, bf16[48,1024]{1,0:T(8,128)(2,1)S(1)}, u32[]{:S(2)}, u32[]{:S(2)}) collective-permute-start(bf16[48,1024]{1,0:T(8,128)(2,1)} %get-tuple-element.334), channel_id=1, source_target_pairs={{0,64},{4,68},{8,72},{12,76},{16,80},{20,84},{24,88},{28,92},{32,9... | collective-permute-start | bytes 294920 | tf_op jit(solution)/shard_map/ppermute | solution.py:28
  20.6 0.0 copy-start
  20.6 0.0 copy-start.1
  20.6 9.4 %conditional.1 = (bf16[48,1024]{1,0:T(8,128)(2,1)}, f32[48,1024]{1,0:T(8,128)S(1)}, s32[2,32,1024]{2,1,0:T(8,128)S(1)}) conditional(s32[]{:T(128)} %bitcast.2, (bf16[48,1024]{1,0:T(8,128)(2,1)}, f32[48,1024]{1,0:T(8,128)S(1)}, s32[4096,1024]{1,0:T(8,128)}) %tuple.124, (bf16[48,1024]{1,0:T(8,128)(2,1)}, ...), branch_computations={%region_0.0_spmd, %region_1.0_spmd, %region_2.0_spmd, %region_3.0_... | conditional | flops 104857600 | bytes 12976192 | solution.py:321
  20.9 3.4 %collective-permute-start.18 = (bf16[48,1024]{1,0:T(8,128)(2,1)}, bf16[48,1024]{1,0:T(8,128)(2,1)}, u32[]{:S(2)}, u32[]{:S(2)}) collective-permute-start(bf16[48,1024]{1,0:T(8,128)(2,1)} %get-tuple-element.264.z_ref), channel_id=1, source_target_pairs={{0,48},{4,52},{8,56},{12,60},{16,64},{20,68},{24,72},{28,76},{32,8... | collective-permute-start | bytes 294920 | tf_op jit(solution)/shard_map/cond/branch_18_fun/ppermute | solution.py:28
  24.3 5.7 %stream.47 = (f32[48,1024]{1,0:T(8,128)S(1)}, s32[2,32,1024]{2,1,0:T(8,128)S(1)}) custom-call(bf16[48,1024]{1,0:T(8,128)(2,1)} %get-tuple-element.264.z_ref, f32[48,1024]{1,0:T(8,128)S(1)} %get-tuple-element.265.self_ref, s32[4096,1024]{1,0:T(8,128)} %get-tuple-element.266.e2_ref), custom_call_target="tpu_custom_call" | custom-call | flops 104857600 | bytes 12582912 | tf_op jit(solution)/shard_map/cond/branch_18_fun/stream/pallas_call | solution.py:298
  30.0 0.0 collective-permute-done.18
  30.0 0.0 collective-permute-done.33.z2_ref
  30.0 0.0 collective-permute-done.32.z1_ref
  30.1 0.0 copy-done
  30.1 0.0 copy-done.1
  30.1 3.1 %second.1 = (f32[1,1024]{1,0:T(1,128)}, f32[32,1,128]{2,1,0:T(1,128)S(1)}) custom-call(bf16[48,1024]{1,0:T(8,128)(2,1)S(1)} %collective-permute-done.32.z1_ref, bf16[48,1024]{1,0:T(8,128)(2,1)S(1)} %collective-permute-done.33.z2_ref, bf16[48,1024]{1,0:T(8,128)(2,1)} %get-tuple-element.337.z3_ref, f32[48,1024]{1,0:T(8,128)S(1)} %get-tuple-element.338.total_ref, ...), custom_call_target="tpu_custom_call" | custom-call | flops 402653184 | bytes 2097152 | tf_op jit(solution)/shard_map/second/pallas_call | solution.py:329
  33.1 11.7 %all_to_all.5 = f32[32,1,128]{2,1,0:T(1,128)S(1)} all-to-all(f32[32,1,128]{2,1,0:T(1,128)S(1)} %get-tuple-element.342), channel_id=1, replica_groups=mesh['node'=32,'feat'=4] {'node'}, dimensions={0} | all-to-all | bytes 32768 | tf_op jit(solution)/shard_map/all_to_all | solution.py:347
  44.8 0.6 %slice_reduce_fusion = f32[]{:T(128)} fusion(f32[32,1,128]{2,1,0:T(1,128)S(1)} %all_to_all.5), kind=kLoop, calls=%fused_computation | loop fusion | flops 31 | bytes 132 | tf_op jit(solution)/shard_map/reduce_sum | solution.py:348
Async XLA Ops:
  2.1 9.4 %collective-permute-start.31 = (bf16[32,1536]{1,0:T(8,128)(2,1)S(1)}, bf16[32,1536]{1,0:T(8,128)(2,1)S(1)}, u32[]{:S(2)}, u32[]{:S(2)}) collective-permute-start(bf16[32,1536]{1,0:T(8,128)(2,1)S(1)} %get-tuple-element.332.after_ref.p0_ref), channel_id=1, source_target_pairs={{0,1},{1,2},{2,3},{3,0},{4,5},{5,6},{6,7},{7,4},{8,9},{9,10},{10,1... | collective-permute-start | bytes 294920 | tf_op jit(solution)/shard_map/ppermute | solution.py:28
  4.3 7.2 %collective-permute-start.30 = (bf16[32,1536]{1,0:T(8,128)(2,1)S(1)}, bf16[32,1536]{1,0:T(8,128)(2,1)S(1)}, u32[]{:S(2)}, u32[]{:S(2)}) collective-permute-start(bf16[32,1536]{1,0:T(8,128)(2,1)S(1)} %get-tuple-element.332.after_ref.p0_ref), channel_id=1, source_target_pairs={{0,2},{1,3},{2,0},{3,1},{4,6},{5,7},{6,4},{7,5},{8,10},{9,11},{10,... | collective-permute-start | bytes 294920 | tf_op jit(solution)/shard_map/ppermute | solution.py:28
  6.9 4.6 %collective-permute-start.29 = (bf16[32,1536]{1,0:T(8,128)(2,1)S(1)}, bf16[32,1536]{1,0:T(8,128)(2,1)S(1)}, u32[]{:S(2)}, u32[]{:S(2)}) collective-permute-start(bf16[32,1536]{1,0:T(8,128)(2,1)S(1)} %get-tuple-element.332.after_ref.p0_ref), channel_id=1, source_target_pairs={{0,3},{1,0},{2,1},{3,2},{4,7},{5,4},{6,5},{7,6},{8,11},{9,8},{10,9... | collective-permute-start | bytes 294920 | tf_op jit(solution)/shard_map/ppermute | solution.py:28
  14.2 15.8 %collective-permute-start.33 = (bf16[48,1024]{1,0:T(8,128)(2,1)}, bf16[48,1024]{1,0:T(8,128)(2,1)S(1)}, u32[]{:S(2)}, u32[]{:S(2)}) collective-permute-start(bf16[48,1024]{1,0:T(8,128)(2,1)} %get-tuple-element.334), channel_id=1, source_target_pairs={{0,4},{4,8},{8,12},{12,16},{16,20},{20,24},{24,28},{28,32},{32,36}... | collective-permute-start | bytes 294920 | tf_op jit(solution)/shard_map/ppermute | solution.py:28
  17.2 12.8 %collective-permute-start.32 = (bf16[48,1024]{1,0:T(8,128)(2,1)}, bf16[48,1024]{1,0:T(8,128)(2,1)S(1)}, u32[]{:S(2)}, u32[]{:S(2)}) collective-permute-start(bf16[48,1024]{1,0:T(8,128)(2,1)} %get-tuple-element.334), channel_id=1, source_target_pairs={{0,64},{4,68},{8,72},{12,76},{16,80},{20,84},{24,88},{28,92},{32,9... | collective-permute-start | bytes 294920 | tf_op jit(solution)/shard_map/ppermute | solution.py:28
  20.6 9.4 %copy-start = (s32[1024]{0:T(1024)S(1)}, s32[1024]{0:T(1024)}, u32[]{:S(2)}) copy-start(s32[1024]{0:T(1024)} %param.48) | copy-start | bytes 12292
  20.6 9.4 %copy-start.1 = (s32[1,4]{1,0:T(1,128)S(1)}, s32[1,4]{1,0:T(1,128)}, u32[]{:S(2)}) copy-start(s32[1,4]{1,0:T(1,128)} %live_ref.1) | copy-start | bytes 52
  20.9 9.1 %collective-permute-start.18 = (bf16[48,1024]{1,0:T(8,128)(2,1)}, bf16[48,1024]{1,0:T(8,128)(2,1)}, u32[]{:S(2)}, u32[]{:S(2)}) collective-permute-start(bf16[48,1024]{1,0:T(8,128)(2,1)} %get-tuple-element.264.z_ref), channel_id=1, source_target_pairs={{0,48},{4,52},{8,56},{12,60},{16,64},{20,68},{24,72},{28,76},{32,8... | collective-permute-start | bytes 294920 | tf_op jit(solution)/shard_map/cond/branch_18_fun/ppermute | solution.py:28
where the time goes:
time: 45.6 us; the launch traced here: 45.5 us
  Pallas kernels  16.4 us (36%)
  starting transfers between devices  15.1 us (33%)
  blocking collectives  11.7 us (26%)
  between operations  1.38 us (3%)
  other arithmetic  0.63 us (1%)
    ppermute x6, starting transfers between devices, from_ahead(): return lax.ppermute(value, axis, pairs)  15.1 us
    all_to_all x1, blocking collectives, local(): everyone = lax.all_to_all(sums, 'node', 0, 0, tiled=True)  11.7 us
    pallas_call x1, Pallas kernels, with_offset(): pl.pallas_call(stream_kernel, out_shape=(jax.ShapeDtypeStruct((padded, bl...  5.71 us
    pallas_call x1, Pallas kernels, local(): pl.pallas_call(load_kernel, out_shape=(jax.ShapeDtypeStruct(edges_one.sha...  3.51 us
    pallas_call x1, Pallas kernels, local(): pl.pallas_call(functools.partial(second_kernel, classes), out_shape=(jax....  3.06 us
    pallas_call x1, Pallas kernels, local(): pl.pallas_call(functools.partial(first_kernel, rows, hid, classes), out_s...  2.68 us
    pallas_call x1, Pallas kernels, local(): pl.pallas_call(functools.partial(pack_kernel, nodes), out_shape=(jax.Shap...  1.44 us
  transfers between devices with their start and end apart: 6, of which 0 were waited for; matrix products, arithmetic and copies ran while one was open for 0% of the time, Pallas kernels for 20%

commit v1 on v0

v1 whole, which is shorter than its diff:
```python
import functools

import jax
import jax.numpy as jnp
from jax import lax
from jax.experimental import pallas as pl
from jax.experimental.pallas import tpu as pltpu
from jax.sharding import PartitionSpec as P

FAN1 = 25
FAN2 = 10
LANES = 128
WORDS = 32
MIB = 1 << 20

VMEM = pl.BlockSpec(memory_space=pltpu.VMEM)
HBM = pl.BlockSpec(memory_space=pltpu.HBM)
SMEM = pl.BlockSpec(memory_space=pltpu.SMEM)


def in_hbm(value):
    return pltpu.with_memory_space_constraint(value, pltpu.HBM)


def from_ahead(value, axis, steps):
    count = lax.axis_size(axis)
    pairs = [(source, (source - steps) % count) for source in range(count)]
    return lax.ppermute(value, axis, pairs)


def pack_kernel(nodes, *refs):
    sources, (out_ref, off_ref), held, (scr, cat, sems) = refs[:6], refs[6:8], refs[8:14], refs[14:]
    copies = [
        pltpu.make_async_copy(source, place, sems.at[index])
        for index, (source, place) in enumerate(zip(sources, held))
    ]
    for copy in copies:
        copy.start()
    x_ref, ws_ref, wn_ref, us_ref, un_ref, need_ref = held
    rows, cols = x_ref.shape
    hid = ws_ref.shape[1]
    classes, depth = us_ref.shape
    height = out_ref.shape[0]
    side = cols + 2 * hid
    scr[rows:, :] = jnp.zeros((height - rows, side), jnp.float32)
    cat[...] = jnp.zeros_like(cat)
    for copy in copies:
        copy.wait()
    scr[:rows, :cols] = x_ref[...].astype(jnp.float32)
    scr[:rows, cols : cols + hid] = ws_ref[...].astype(jnp.float32)
    scr[:rows, cols + hid :] = wn_ref[...].astype(jnp.float32)
    cat[:classes, :depth] = us_ref[...].astype(jnp.float32)
    cat[LANES // 2 : LANES // 2 + classes, :depth] = un_ref[...].astype(jnp.float32)
    by_unit = cat[...].T
    out_ref[:, :side] = scr[...].astype(jnp.bfloat16)
    for piece in range(depth // height):
        place = slice(side + piece * LANES, side + (piece + 1) * LANES)
        out_ref[:, place] = by_unit[piece * height : (piece + 1) * height].astype(jnp.bfloat16)
    offset = lax.rem(need_ref[0, 3] - lax.axis_index("node") + nodes, nodes)
    off_ref[0] = offset - 1 - (offset > nodes // 2).astype(jnp.int32)


def packed_bits(piece, first_bit):
    words = None
    for group in range(piece.shape[0] // WORDS):
        bits = piece[group * WORDS : (group + 1) * WORDS, :] << (first_bit + group)
        words = bits if words is None else words | bits
    return words


def load_kernel(e1_ref, e2_ref, after_ref, e1_out, bits_ref, held, sems):
    pieces, rows = held.shape[0] // 2, held.shape[1]
    base = e1_ref.shape[0]
    copies = []
    for index in range(2 * pieces):
        ref, first = (e1_ref, 0) if index < pieces else (e2_ref, base)
        source = ref.at[pl.ds(first + index % pieces * rows, rows)]
        copies.append(pltpu.make_async_copy(source, held.at[index], sems.at[index]))
    for copy in copies:
        copy.start()
    for index in range(pieces):
        copies[index].wait()
        e1_out[index * rows : (index + 1) * rows, :] = (
            held[index].astype(jnp.float32).astype(jnp.bfloat16)
        )
    words = jnp.zeros(bits_ref.shape, jnp.int32)
    for index in range(pieces):
        copies[pieces + index].wait()
        words = words | packed_bits(held.at[pieces + index], index * (rows // WORDS))
    bits_ref[...] = words


def stream_kernel(z_ref, self_ref, e2_ref, total_ref, bits_ref, held, acc, sems):
    rows = held.shape[1]
    cols = z_ref.shape[1]
    pieces = cols // rows
    sources = [slot * pieces + index for slot in (0, 2) for index in range(pieces)]
    copies = [
        pltpu.make_async_copy(e2_ref.at[pl.ds(source * rows, rows)], held.at[index], sems.at[index])
        for index, source in enumerate(sources)
    ]
    for copy in copies:
        copy.start()
    acc[...] = jnp.zeros_like(acc)

    def arrived(index):
        pltpu.make_async_copy(e2_ref.at[pl.ds(0, rows)], held.at[index], sems.at[index]).wait()
        return held.at[index]

    @pl.loop(0, pieces)
    def _(index):
        adjacency = arrived(index)[...].astype(jnp.float32).astype(jnp.bfloat16)
        own = z_ref[:, pl.ds(pl.multiple_of(index * rows, rows), rows)]
        acc[...] += jnp.dot(own, adjacency, preferred_element_type=jnp.float32)

    total_ref[...] = self_ref[...] + acc[...] / FAN2
    bits_ref[...] = jnp.zeros_like(bits_ref)

    @pl.loop(pieces, 2 * pieces)
    def _(index):
        first_bit = (index - pieces) * (rows // WORDS)
        bits_ref[...] = bits_ref[...] | packed_bits(arrived(index), first_bit)


def first_kernel(
    hid, depth, p0_ref, p1_ref, p2_ref, p3_ref, e_ref, self_ref, z_ref, send_ref, own_ref, x, w1, w2
):
    me = lax.axis_index("feat")
    height = p0_ref.shape[0]
    cols = x.shape[1]
    feats = x.shape[0] // height
    padded = z_ref.shape[0]
    for step, ref in enumerate((p0_ref, p1_ref, p2_ref, p3_ref)):
        place = lax.rem(me + step, feats)
        rows = pl.ds(pl.multiple_of(place * height, height), height)
        x[rows, :] = ref[:, :cols]
        w1[rows, :] = ref[:, cols : cols + hid]
        below = pl.ds(pl.multiple_of((feats + place) * height, height), height)
        w1[below, :] = ref[:, cols + hid : cols + 2 * hid]
        for piece in range(depth // height):
            units = pl.ds(pl.multiple_of(place * depth + piece * height, height), height)
            lanes = slice(cols + 2 * hid + piece * LANES, cols + 2 * hid + (piece + 1) * LANES)
            w2[units, :] = ref[:, lanes]
    inputs = x[...]
    weights = w1[...].astype(jnp.float32).T.astype(jnp.bfloat16)
    project = w2[...].astype(jnp.float32).T.astype(jnp.bfloat16)
    chunk = 256
    for first in range(0, cols, chunk):
        part = slice(first, first + chunk)
        nbr = jnp.dot(inputs, e_ref[:, part], preferred_element_type=jnp.float32) / FAN1
        stacked = jnp.concatenate([inputs[:, part], nbr.astype(jnp.bfloat16)], axis=0)
        before = jnp.dot(weights, stacked, preferred_element_type=jnp.float32)
        hidden = jnp.maximum(before, 0.0).astype(jnp.bfloat16)
        both = jnp.dot(project, hidden, preferred_element_type=jnp.float32)
        self_ref[:, part] = both[:padded]
        z = both[LANES // 2 : LANES // 2 + padded].astype(jnp.bfloat16)
        z_ref[:, part] = z
        send_ref[:, part] = z
        own_ref[:, part] = z


def second_kernel(
    classes,
    z1_ref,
    z2_ref,
    z3_hbm,
    total_ref,
    live_ref,
    b1_ref,
    b2_ref,
    e2_ref,
    label_ref,
    loss_ref,
    sum_ref,
    zs,
    z3_ref,
    held,
    acc,
    sems,
):
    padded, cols = total_ref.shape
    pieces, rows = held.shape[0], held.shape[1]
    fetch = pltpu.make_async_copy(z3_hbm, z3_ref, sems.at[pieces])
    fetch.start()
    copies = [
        pltpu.make_async_copy(
            e2_ref.at[pl.ds(3 * cols + index * rows, rows)], held.at[index], sems.at[index]
        )
        for index in range(pieces)
    ]
    for copy in copies:
        copy.start()
    chunk = 256
    group = lax.broadcasted_iota(jnp.int32, (1, cols), 1) // WORDS
    scale = jnp.ones((1, cols), jnp.float32)
    for bit in range(5):
        scale = scale * jnp.where((group >> bit) % 2 == 1, 2.0 ** -(1 << bit), 1.0)
    scale = jnp.where(group == 31, -scale, scale)
    for slot, ref in enumerate((z1_ref, z2_ref)):
        used = jnp.where(live_ref[0, slot + 1] == 1, scale, 0.0)
        zs[:, slot * cols : (slot + 1) * cols] = (ref[...].astype(jnp.float32) * used).astype(
            jnp.bfloat16
        )
    for first in range(0, cols, chunk):
        part = slice(first, first + chunk)
        planes = []
        for words in (b1_ref[:, part], b2_ref[:, part]):
            for bit in range(32):
                mask = (1 << bit) if bit < 31 else -(1 << 31)
                planes.append((words & jnp.int32(mask)).astype(jnp.float32).astype(jnp.bfloat16))
        adjacency = jnp.concatenate(planes, axis=0)
        acc[:, part] = jnp.dot(zs[...], adjacency, preferred_element_type=jnp.float32)
    fetch.wait()
    for copy in copies:
        copy.wait()
    live = jnp.where(live_ref[0, 3] == 1, 1.0, 0.0)
    fourth = (z3_ref[...].astype(jnp.float32) * live).astype(jnp.bfloat16)
    class_ids = lax.broadcasted_iota(jnp.int32, (padded, chunk), 0)
    summed = jnp.zeros((1, chunk), jnp.float32)
    for first in range(0, cols, chunk):
        part = slice(first, first + chunk)
        adjacency = held[:, :, part].reshape(cols, chunk)
        adjacency = adjacency.astype(jnp.float32).astype(jnp.bfloat16)
        term = acc[:, part] + jnp.dot(fourth, adjacency, preferred_element_type=jnp.float32)
        logits = total_ref[:, part] + term / FAN2
        powers = jnp.where(class_ids < classes, jnp.exp(logits), 0.0)
        picked = jnp.where(class_ids == label_ref[:, part], logits, 0.0)
        loss = jnp.log(jnp.sum(powers, 0, keepdims=True)) - jnp.sum(picked, 0, keepdims=True)
        loss_ref[:, part] = loss
        summed = summed + loss
    mean = jnp.sum(summed, keepdims=True) / (cols * sum_ref.shape[0])
    sum_ref[...] = jnp.broadcast_to(mean.reshape(1, 1, 1), sum_ref.shape)


def local(
    features,
    edges_one,
    w1_self,
    w1_nbr,
    need_blocks,
    live_slots,
    edges_two,
    w2_self,
    w2_nbr,
    labels,
):
    rows, block_len = features.shape
    hid = w1_self.shape[1]
    depth, classes = w2_self.shape
    nodes = lax.axis_size("node")
    feats = lax.axis_size("feat")
    height = pl.cdiv(rows, 8) * 8
    width = block_len + 2 * hid + depth // height * LANES
    padded = pl.cdiv(classes, 16) * 16

    packed, number = pl.pallas_call(
        functools.partial(pack_kernel, nodes),
        out_shape=(
            jax.ShapeDtypeStruct((height, width), jnp.bfloat16),
            jax.ShapeDtypeStruct((1,), jnp.int32),
        ),
        in_specs=[HBM] * 6,
        out_specs=(VMEM, SMEM),
        scratch_shapes=[
            pltpu.VMEM((rows, block_len), jnp.bfloat16),
            pltpu.VMEM((rows, hid), jnp.bfloat16),
            pltpu.VMEM((rows, hid), jnp.bfloat16),
            pltpu.VMEM((classes, depth), jnp.bfloat16),
            pltpu.VMEM((classes, depth), jnp.bfloat16),
            pltpu.SMEM(need_blocks.shape, jnp.int32),
            pltpu.VMEM((height, block_len + 2 * hid), jnp.float32),
            pltpu.VMEM((LANES, LANES), jnp.float32),
            pltpu.SemaphoreType.DMA((6,)),
        ],
        compiler_params=pltpu.CompilerParams(vmem_limit_bytes=4 * MIB),
        cost_estimate=pl.CostEstimate(flops=2 * MIB, bytes_accessed=MIB // 4, transcendentals=0),
        name="pack",
    )(*map(in_hbm, (features, w1_self, w1_nbr, w2_self.T, w2_nbr.T, need_blocks)))

    blocks = [packed] + [from_ahead(packed, "feat", step) for step in range(1, feats)]
    words = block_len // 32
    edges_one, bits_one = pl.pallas_call(
        load_kernel,
        out_shape=(
            jax.ShapeDtypeStruct(edges_one.shape, jnp.bfloat16),
            jax.ShapeDtypeStruct((words, block_len), jnp.int32),
        ),
        in_specs=[HBM, HBM, VMEM],
        out_specs=(VMEM, VMEM),
        scratch_shapes=[
            pltpu.VMEM((8, block_len // 4, block_len), jnp.int32),
            pltpu.SemaphoreType.DMA((8,)),
        ],
        compiler_params=pltpu.CompilerParams(vmem_limit_bytes=12 * MIB),
        cost_estimate=pl.CostEstimate(flops=100 * MIB, bytes_accessed=8 * MIB, transcendentals=0),
        name="load",
    )(in_hbm(edges_one), in_hbm(edges_two), packed)

    self_term, mine, send, own = pl.pallas_call(
        functools.partial(first_kernel, hid, depth),
        out_shape=(
            jax.ShapeDtypeStruct((padded, block_len), jnp.float32),
            jax.ShapeDtypeStruct((padded, block_len), jnp.bfloat16),
            jax.ShapeDtypeStruct((padded, block_len), jnp.bfloat16),
            jax.ShapeDtypeStruct((padded, block_len), jnp.bfloat16),
        ),
        in_specs=[VMEM] * 5,
        out_specs=(VMEM,) * 4,
        scratch_shapes=[
            pltpu.VMEM((feats * height, block_len), jnp.bfloat16),
            pltpu.VMEM((2 * feats * height, hid), jnp.bfloat16),
            pltpu.VMEM((feats * depth, LANES), jnp.bfloat16),
        ],
        compiler_params=pltpu.CompilerParams(vmem_limit_bytes=16 * MIB),
        cost_estimate=pl.CostEstimate(
            flops=2 * 128 * block_len * block_len, bytes_accessed=4 * MIB, transcendentals=0
        ),
        name="first",
    )(*blocks, edges_one)

    half = from_ahead(mine, "node", nodes // 2)
    behind = from_ahead(mine, "node", nodes - 1)

    def with_offset(step, send, own, self_term, edges_two):
        fourth = from_ahead(send, "node", step)
        total, bits_two = pl.pallas_call(
            stream_kernel,
            out_shape=(
                jax.ShapeDtypeStruct((padded, block_len), jnp.float32),
                jax.ShapeDtypeStruct((words, block_len), jnp.int32),
            ),
            in_specs=[VMEM, VMEM, HBM],
            out_specs=(VMEM, VMEM),
            scratch_shapes=[
                pltpu.VMEM((8, block_len // 4, block_len), jnp.int32),
                pltpu.VMEM((padded, block_len), jnp.float32),
                pltpu.SemaphoreType.DMA((8,)),
            ],
            compiler_params=pltpu.CompilerParams(vmem_limit_bytes=12 * MIB),
            cost_estimate=pl.CostEstimate(
                flops=100 * MIB, bytes_accessed=8 * MIB, transcendentals=0
            ),
            name="stream",
        )(own, self_term, in_hbm(edges_two))
        return fourth, total, bits_two

    taken = (0, nodes // 2, nodes - 1)
    steps = [step for step in range(nodes) if step not in taken]
    fourth, total, bits_two = lax.switch(
        number[0],
        [functools.partial(with_offset, step) for step in steps],
        send,
        own,
        self_term,
        edges_two,
    )

    loss, sums = pl.pallas_call(
        functools.partial(second_kernel, classes),
        out_shape=(
            jax.ShapeDtypeStruct((1, block_len), jnp.float32),
            jax.ShapeDtypeStruct((nodes, 1, LANES), jnp.float32),
        ),
        in_specs=[VMEM, VMEM, HBM, VMEM, SMEM, VMEM, VMEM, HBM, VMEM],
        out_specs=(VMEM, VMEM),
        scratch_shapes=[
            pltpu.VMEM((padded, 2 * block_len), jnp.bfloat16),
            pltpu.VMEM((padded, block_len), jnp.bfloat16),
            pltpu.VMEM((4, block_len // 4, block_len), jnp.int32),
            pltpu.VMEM((padded, block_len), jnp.float32),
            pltpu.SemaphoreType.DMA((5,)),
        ],
        compiler_params=pltpu.CompilerParams(vmem_limit_bytes=16 * MIB),
        cost_estimate=pl.CostEstimate(
            flops=2 * 64 * 3 * block_len * block_len,
            bytes_accessed=2 * MIB,
            transcendentals=padded * block_len,
        ),
        name="second",
    )(
        half,
        behind,
        in_hbm(fourth),
        total,
        live_slots,
        bits_one,
        bits_two,
        in_hbm(edges_two),
        labels[None, :],
    )

    everyone = lax.all_to_all(sums, "node", 0, 0, tiled=True)
    mean_loss = jnp.sum(everyone[:, 0, 0])
    return (loss[0], mean_loss)


def solution(mesh):
    return jax.shard_map(
        local,
        mesh=mesh,
        in_specs=(
            P("feat", "node"),
            P(None, "node"),
            P("feat", None),
            P("feat", None),
            P("node", None),
            P("node", None),
            P(None, "node"),
            P("feat", None),
            P("feat", None),
            P("node"),
        ),
        out_specs=(P("node"), P()),
        check_vma=False,
    )
```

time: 45.6 us -> 45.2 us (level); the launches traced: 45.5 us -> 44.3 us
  starting transfers between devices: 15.1 us -> 12.7 us
  blocking collectives: 11.7 us -> 13.9 us
  Pallas kernels: 16.4 us -> 15.1 us
    ppermute x6, starting transfers between devices: 15.1 us -> 12.7 us  [from_ahead(): return lax.ppermute(value, axis, pairs)]
    all_to_all x1, blocking collectives: 11.7 us -> 13.9 us  [local(): everyone = lax.all_to_all(sums, 'node', 0, 0, tiled=True)]
    pallas_call x1, Pallas kernels: 5.71 us -> 3.55 us  [with_offset(): pl.pallas_call(stream_kernel, out_shape=(jax.ShapeDtypeStruct((padded, bl...]
    pallas_call x1, Pallas kernels: 3.06 us -> 4.52 us  [local(): pl.pallas_call(functools.partial(second_kernel, classes), out_shape=(jax....]
    pallas_call x1, Pallas kernels: 2.68 us -> 2.04 us  [local(): pl.pallas_call(functools.partial(first_kernel, hid, depth), out_shape=(ja...]
  transfers between devices with their start and end apart: 6 -> 6, of which waited for: 0 -> 1; matrix products, arithmetic and copies ran while one was open for 0% -> 0% of each run, Pallas kernels for 20% -> 16%
where the time goes in v1:
time: 45.2 us; the launch traced here: 44.3 us
  Pallas kernels  15.1 us (33%)
  blocking collectives  13.9 us (31%)
  starting transfers between devices  12.7 us (28%)
  between operations  1.38 us (3%)
  other arithmetic  0.63 us (1%)
    all_to_all x1, blocking collectives, local(): everyone = lax.all_to_all(sums, 'node', 0, 0, tiled=True)  13.9 us
    ppermute x6, starting transfers between devices, from_ahead(): return lax.ppermute(value, axis, pairs)  12.7 us
    pallas_call x1, Pallas kernels, local(): pl.pallas_call(functools.partial(second_kernel, classes), out_shape=(jax....  4.52 us
    pallas_call x1, Pallas kernels, local(): pl.pallas_call(load_kernel, out_shape=(jax.ShapeDtypeStruct(edges_one.sha...  3.57 us
    pallas_call x1, Pallas kernels, with_offset(): pl.pallas_call(stream_kernel, out_shape=(jax.ShapeDtypeStruct((padded, bl...  3.55 us
    pallas_call x1, Pallas kernels, local(): pl.pallas_call(functools.partial(first_kernel, hid, depth), out_shape=(ja...  2.04 us
    pallas_call x1, Pallas kernels, local(): pl.pallas_call(functools.partial(pack_kernel, nodes), out_shape=(jax.Shap...  1.45 us
  transfers between devices with their start and end apart: 6, of which 1 were waited for; matrix products, arithmetic and copies ran while one was open for 0% of the time, Pallas kernels for 16%

profile of v1, /device:TPU:1, one launch (start us, length us, event | category | flops | bytes accessed | tf_op | source)
XLA Modules:
  0.0 44.3 jit_solution(7808906354570562634)
XLA Ops:
  0.6 1.4 %pack.1 = (bf16[32,1792]{1,0:T(8,128)(2,1)S(1)}, s32[1]{0:T(128)}) custom-call(bf16[25,1024]{1,0:T(8,128)(2,1)} %refs_0_.1, bf16[25,256]{1,0:T(8,128)(2,1)} %refs_1_.1, bf16[25,256]{1,0:T(8,128)(2,1)} %refs_2_.1, bf16[47,64]{1,0:T(8,128)(2,1)} %bitcast.6, bf16[47,64]{1,0:T(8,128)(2,1)} %bitcast.7, s32[1,4]{1,0:T(1,128)} %refs_5_.1), custom_call_target="tpu_custom_call" | custom-call | flops 2097152 | bytes 262144 | tf_op jit(solution)/shard_map/pack/pallas_call | solution.py:256
  2.1 2.2 %collective-permute-start.31 = (bf16[32,1792]{1,0:T(8,128)(2,1)S(1)}, bf16[32,1792]{1,0:T(8,128)(2,1)S(1)}, u32[]{:S(2)}, u32[]{:S(2)}) collective-permute-start(bf16[32,1792]{1,0:T(8,128)(2,1)S(1)} %get-tuple-element.421.after_ref.p0_ref), channel_id=1, source_target_pairs={{0,1},{1,2},{2,3},{3,0},{4,5},{5,6},{6,7},{7,4},{8,9},{9,10},{10,1... | collective-permute-start | bytes 344072 | tf_op jit(solution)/shard_map/ppermute | solution.py:28
  4.3 2.6 %collective-permute-start.30 = (bf16[32,1792]{1,0:T(8,128)(2,1)S(1)}, bf16[32,1792]{1,0:T(8,128)(2,1)S(1)}, u32[]{:S(2)}, u32[]{:S(2)}) collective-permute-start(bf16[32,1792]{1,0:T(8,128)(2,1)S(1)} %get-tuple-element.421.after_ref.p0_ref), channel_id=1, source_target_pairs={{0,2},{1,3},{2,0},{3,1},{4,6},{5,7},{6,4},{7,5},{8,10},{9,11},{10,... | collective-permute-start | bytes 344072 | tf_op jit(solution)/shard_map/ppermute | solution.py:28
  6.9 1.1 %collective-permute-start.29 = (bf16[32,1792]{1,0:T(8,128)(2,1)S(1)}, bf16[32,1792]{1,0:T(8,128)(2,1)S(1)}, u32[]{:S(2)}, u32[]{:S(2)}) collective-permute-start(bf16[32,1792]{1,0:T(8,128)(2,1)S(1)} %get-tuple-element.421.after_ref.p0_ref), channel_id=1, source_target_pairs={{0,3},{1,0},{2,1},{3,2},{4,7},{5,4},{6,5},{7,6},{8,11},{9,8},{10,9... | collective-permute-start | bytes 344072 | tf_op jit(solution)/shard_map/ppermute | solution.py:28
  8.0 3.6 %load.1 = (bf16[1024,1024]{1,0:T(8,128)(2,1)S(1)}, s32[32,1024]{1,0:T(8,128)S(1)}) custom-call(s32[1024,1024]{1,0:T(8,128)} %e1_ref.1, s32[4096,1024]{1,0:T(8,128)} %e2_ref.3, bf16[32,1792]{1,0:T(8,128)(2,1)S(1)} %get-tuple-element.421.after_ref.p0_ref), custom_call_target="tpu_custom_call" | custom-call | flops 104857600 | bytes 8388608 | tf_op jit(solution)/shard_map/load/pallas_call | solution.py:282
  11.5 0.0 collective-permute-done.31.p3_ref
  11.5 0.4 collective-permute-done.30.p2_ref
  11.9 0.0 collective-permute-done.29.p1_ref
  11.9 2.0 %first.1 = (f32[48,1024]{1,0:T(8,128)S(1)}, bf16[48,1024]{1,0:T(8,128)(2,1)S(1)}, bf16[48,1024]{1,0:T(8,128)(2,1)S(1)}, bf16[48,1024]{1,0:T(8,128)(2,1)S(1)}) custom-call(bf16[32,1792]{1,0:T(8,128)(2,1)S(1)} %get-tuple-element.421.after_ref.p0_ref, bf16[32,1792]{1,0:T(8,128)(2,1)S(1)} %collective-permute-done.29.p1_ref, ...), custom_call_target="tpu_custom_call" | custom-call | flops 268435456 | bytes 4194304 | tf_op jit(solution)/shard_map/first/pallas_call | solution.py:299
  14.0 3.1 %collective-permute-start.33 = (bf16[48,1024]{1,0:T(8,128)(2,1)S(1)}, bf16[48,1024]{1,0:T(8,128)(2,1)S(1)}, u32[]{:S(2)}, u32[]{:S(2)}) collective-permute-start(bf16[48,1024]{1,0:T(8,128)(2,1)S(1)} %get-tuple-element.423), channel_id=1, source_target_pairs={{0,4},{4,8},{8,12},{12,16},{16,20},{20,24},{24,28},{28,32},{32,36}... | collective-permute-start | bytes 294920 | tf_op jit(solution)/shard_map/ppermute | solution.py:28
  17.1 2.7 %collective-permute-start.32 = (bf16[48,1024]{1,0:T(8,128)(2,1)S(1)}, bf16[48,1024]{1,0:T(8,128)(2,1)S(1)}, u32[]{:S(2)}, u32[]{:S(2)}) collective-permute-start(bf16[48,1024]{1,0:T(8,128)(2,1)S(1)} %get-tuple-element.423), channel_id=1, source_target_pairs={{0,64},{4,68},{8,72},{12,76},{16,80},{20,84},{24,88},{28,92},{32,9... | collective-permute-start | bytes 294920 | tf_op jit(solution)/shard_map/ppermute | solution.py:28
  20.5 0.0 copy-start
  20.5 0.0 copy-start.1
  20.5 4.7 %conditional.1 = (bf16[48,1024]{1,0:T(8,128)(2,1)}, f32[48,1024]{1,0:T(8,128)S(1)}, s32[32,1024]{1,0:T(8,128)S(1)}) conditional(s32[]{:T(128)} %bitcast.2, (bf16[48,1024]{1,0:T(8,128)(2,1)S(1)}, bf16[48,1024]{1,0:T(8,128)(2,1)S(1)}, f32[48,1024]{1,0:T(8,128)S(1)}, s32[4096,1024]{1,0:T(8,128)}) %tuple.124, ...), branch_computations={%region_0.0_spmd, %region_1.0_spmd, %region_2.0_spmd, %region_3.0_... | conditional | flops 104857600 | bytes 8781888 | solution.py:349
  20.5 0.9 %collective-permute-start.7 = (bf16[48,1024]{1,0:T(8,128)(2,1)S(1)}, bf16[48,1024]{1,0:T(8,128)(2,1)}, u32[]{:S(2)}, u32[]{:S(2)}) collective-permute-start(bf16[48,1024]{1,0:T(8,128)(2,1)S(1)} %get-tuple-element.274), channel_id=1, source_target_pairs={{0,96},{4,100},{8,104},{12,108},{16,112},{20,116},{24,120},{28,124... | collective-permute-start | bytes 294920 | tf_op jit(solution)/shard_map/cond/branch_7_fun/ppermute | solution.py:28
  21.5 3.5 %stream.36 = (f32[48,1024]{1,0:T(8,128)S(1)}, s32[32,1024]{1,0:T(8,128)S(1)}) custom-call(bf16[48,1024]{1,0:T(8,128)(2,1)S(1)} %get-tuple-element.275.z_ref, f32[48,1024]{1,0:T(8,128)S(1)} %get-tuple-element.276.self_ref, s32[4096,1024]{1,0:T(8,128)} %get-tuple-element.277.e2_ref), custom_call_target="tpu_custom_call" | custom-call | flops 104857600 | bytes 8388608 | tf_op jit(solution)/shard_map/cond/branch_7_fun/stream/pallas_call | solution.py:326
  25.0 0.0 collective-permute-done.7
  25.2 0.0 collective-permute-done.33.z2_ref
  25.3 0.0 collective-permute-done.32.z1_ref
  25.3 0.0 copy-done
  25.3 0.0 copy-done.1
  25.3 4.5 %second.1 = (f32[1,1024]{1,0:T(1,128)}, f32[32,1,128]{2,1,0:T(1,128)S(1)}) custom-call(bf16[48,1024]{1,0:T(8,128)(2,1)S(1)} %collective-permute-done.32.z1_ref, bf16[48,1024]{1,0:T(8,128)(2,1)S(1)} %collective-permute-done.33.z2_ref, bf16[48,1024]{1,0:T(8,128)(2,1)} %get-tuple-element.428.z3_hbm, f32[48,1024]{1,0:T(8,128)S(1)} %get-tuple-element.429.total_ref, ...), custom_call_target="tpu_custom_call" | custom-call | flops 402653184 | bytes 2097152 | tf_op jit(solution)/shard_map/second/pallas_call | solution.py:358
  29.8 13.9 %all_to_all.5 = f32[32,1,128]{2,1,0:T(1,128)S(1)} all-to-all(f32[32,1,128]{2,1,0:T(1,128)S(1)} %get-tuple-element.433), channel_id=1, replica_groups=mesh['node'=32,'feat'=4] {'node'}, dimensions={0} | all-to-all | bytes 32768 | tf_op jit(solution)/shard_map/all_to_all | solution.py:392
  43.7 0.6 %slice_reduce_fusion = f32[]{:T(128)} fusion(f32[32,1,128]{2,1,0:T(1,128)S(1)} %all_to_all.5), kind=kLoop, calls=%fused_computation | loop fusion | flops 31 | bytes 132 | tf_op jit(solution)/shard_map/reduce_sum | solution.py:393
Async XLA Ops:
  2.1 9.5 %collective-permute-start.31 = (bf16[32,1792]{1,0:T(8,128)(2,1)S(1)}, bf16[32,1792]{1,0:T(8,128)(2,1)S(1)}, u32[]{:S(2)}, u32[]{:S(2)}) collective-permute-start(bf16[32,1792]{1,0:T(8,128)(2,1)S(1)} %get-tuple-element.421.after_ref.p0_ref), channel_id=1, source_target_pairs={{0,1},{1,2},{2,3},{3,0},{4,5},{5,6},{6,7},{7,4},{8,9},{9,10},{10,1... | collective-permute-start | bytes 344072 | tf_op jit(solution)/shard_map/ppermute | solution.py:28
  4.3 7.6 %collective-permute-start.30 = (bf16[32,1792]{1,0:T(8,128)(2,1)S(1)}, bf16[32,1792]{1,0:T(8,128)(2,1)S(1)}, u32[]{:S(2)}, u32[]{:S(2)}) collective-permute-start(bf16[32,1792]{1,0:T(8,128)(2,1)S(1)} %get-tuple-element.421.after_ref.p0_ref), channel_id=1, source_target_pairs={{0,2},{1,3},{2,0},{3,1},{4,6},{5,7},{6,4},{7,5},{8,10},{9,11},{10,... | collective-permute-start | bytes 344072 | tf_op jit(solution)/shard_map/ppermute | solution.py:28
  6.9 5.0 %collective-permute-start.29 = (bf16[32,1792]{1,0:T(8,128)(2,1)S(1)}, bf16[32,1792]{1,0:T(8,128)(2,1)S(1)}, u32[]{:S(2)}, u32[]{:S(2)}) collective-permute-start(bf16[32,1792]{1,0:T(8,128)(2,1)S(1)} %get-tuple-element.421.after_ref.p0_ref), channel_id=1, source_target_pairs={{0,3},{1,0},{2,1},{3,2},{4,7},{5,4},{6,5},{7,6},{8,11},{9,8},{10,9... | collective-permute-start | bytes 344072 | tf_op jit(solution)/shard_map/ppermute | solution.py:28
  14.0 11.3 %collective-permute-start.33 = (bf16[48,1024]{1,0:T(8,128)(2,1)S(1)}, bf16[48,1024]{1,0:T(8,128)(2,1)S(1)}, u32[]{:S(2)}, u32[]{:S(2)}) collective-permute-start(bf16[48,1024]{1,0:T(8,128)(2,1)S(1)} %get-tuple-element.423), channel_id=1, source_target_pairs={{0,4},{4,8},{8,12},{12,16},{16,20},{20,24},{24,28},{28,32},{32,36}... | collective-permute-start | bytes 294920 | tf_op jit(solution)/shard_map/ppermute | solution.py:28
  17.1 8.2 %collective-permute-start.32 = (bf16[48,1024]{1,0:T(8,128)(2,1)S(1)}, bf16[48,1024]{1,0:T(8,128)(2,1)S(1)}, u32[]{:S(2)}, u32[]{:S(2)}) collective-permute-start(bf16[48,1024]{1,0:T(8,128)(2,1)S(1)} %get-tuple-element.423), channel_id=1, source_target_pairs={{0,64},{4,68},{8,72},{12,76},{16,80},{20,84},{24,88},{28,92},{32,9... | collective-permute-start | bytes 294920 | tf_op jit(solution)/shard_map/ppermute | solution.py:28
  20.5 4.8 %copy-start = (s32[1024]{0:T(1024)S(1)}, s32[1024]{0:T(1024)}, u32[]{:S(2)}) copy-start(s32[1024]{0:T(1024)} %param.48) | copy-start | bytes 12292
  20.5 4.8 %copy-start.1 = (s32[1,4]{1,0:T(1,128)S(1)}, s32[1,4]{1,0:T(1,128)}, u32[]{:S(2)}) copy-start(s32[1,4]{1,0:T(1,128)} %live_ref.1) | copy-start | bytes 52
  20.5 4.5 %collective-permute-start.7 = (bf16[48,1024]{1,0:T(8,128)(2,1)S(1)}, bf16[48,1024]{1,0:T(8,128)(2,1)}, u32[]{:S(2)}, u32[]{:S(2)}) collective-permute-start(bf16[48,1024]{1,0:T(8,128)(2,1)S(1)} %get-tuple-element.274), channel_id=1, source_target_pairs={{0,96},{4,100},{8,104},{12,108},{16,112},{20,116},{24,120},{28,124... | collective-permute-start | bytes 294920 | tf_op jit(solution)/shard_map/cond/branch_7_fun/ppermute | solution.py:28

commit v2 on v1

v2 whole, which is shorter than its diff:
```python
import functools

import jax
import jax.numpy as jnp
from jax import lax
from jax.experimental import pallas as pl
from jax.experimental.pallas import tpu as pltpu
from jax.sharding import PartitionSpec as P

FAN1 = 25
FAN2 = 10
LANES = 128
WORDS = 32
MIB = 1 << 20

VMEM = pl.BlockSpec(memory_space=pltpu.VMEM)
HBM = pl.BlockSpec(memory_space=pltpu.HBM)
SMEM = pl.BlockSpec(memory_space=pltpu.SMEM)


def in_hbm(value):
    return pltpu.with_memory_space_constraint(value, pltpu.HBM)


def from_ahead(value, axis, steps):
    count = lax.axis_size(axis)
    pairs = [(source, (source - steps) % count) for source in range(count)]
    return lax.ppermute(value, axis, pairs)


def pack_kernel(*refs):
    sources, (out_ref, edges_ref), held, (scr, cat, sems) = refs[:6], refs[6:8], refs[8:13], refs[13:]
    copies = [
        pltpu.make_async_copy(source, place, sems.at[index])
        for index, (source, place) in enumerate(zip(sources[:5], held))
    ]
    ahead = sources[5].at[pl.ds(0, edges_ref.shape[0])]
    copies.append(pltpu.make_async_copy(ahead, edges_ref, sems.at[5]))
    for copy in copies:
        copy.start()
    x_ref, ws_ref, wn_ref, us_ref, un_ref = held
    rows, cols = x_ref.shape
    hid = ws_ref.shape[1]
    classes, depth = us_ref.shape
    height = out_ref.shape[0]
    side = cols + 2 * hid
    scr[rows:, :] = jnp.zeros((height - rows, side), jnp.float32)
    cat[...] = jnp.zeros_like(cat)
    for copy in copies[:5]:
        copy.wait()
    scr[:rows, :cols] = x_ref[...].astype(jnp.float32)
    scr[:rows, cols : cols + hid] = ws_ref[...].astype(jnp.float32)
    scr[:rows, cols + hid :] = wn_ref[...].astype(jnp.float32)
    cat[:classes, :depth] = us_ref[...].astype(jnp.float32)
    cat[LANES // 2 : LANES // 2 + classes, :depth] = un_ref[...].astype(jnp.float32)
    by_unit = cat[...].T
    out_ref[:, :side] = scr[...].astype(jnp.bfloat16)
    for piece in range(depth // height):
        place = slice(side + piece * LANES, side + (piece + 1) * LANES)
        out_ref[:, place] = by_unit[piece * height : (piece + 1) * height].astype(jnp.bfloat16)
    copies[5].wait()


def packed_bits(piece, first_bit):
    words = None
    for group in range(piece.shape[0] // WORDS):
        bits = piece[group * WORDS : (group + 1) * WORDS, :] << (first_bit + group)
        words = bits if words is None else words | bits
    return words


def load_kernel(
    nodes, e1_ref, ready_ref, e2_ref, need_ref, live_ref, e1_out, bits_ref, number_ref, need, live, held, sems
):
    pieces, rows = bits_ref.shape[0] * 4, held.shape[1]
    cols = e1_out.shape[0]
    done = ready_ref.shape[0]
    sources = [e1_ref.at[pl.ds(first, rows)] for first in range(done, cols, rows)]
    before = len(sources)
    for slot in (1, 3):
        sources += [e2_ref.at[pl.ds(first, rows)] for first in range(slot * cols, (slot + 1) * cols, rows)]
    copies = [
        pltpu.make_async_copy(source, held.at[index], sems.at[index])
        for index, source in enumerate(sources)
    ]
    small = [
        pltpu.make_async_copy(need_ref, need, sems.at[len(sources)]),
        pltpu.make_async_copy(live_ref, live, sems.at[len(sources) + 1]),
    ]
    for copy in small + copies:
        copy.start()
    e1_out[:done, :] = ready_ref[...].astype(jnp.float32).astype(jnp.bfloat16)
    for copy in small:
        copy.wait()
    offset = lax.rem(need[0, 3] - lax.axis_index("node") + nodes, nodes)
    number_ref[0] = offset - 1 - (offset > nodes // 2).astype(jnp.int32)
    for index in range(before):
        copies[index].wait()
        first = done + index * rows
        e1_out[first : first + rows, :] = held[index].astype(jnp.float32).astype(jnp.bfloat16)
    per_slot = cols // rows
    for place, slot in enumerate((1, 3)):
        words = jnp.zeros(bits_ref.shape[1:], jnp.int32)
        for index in range(per_slot):
            at = before + place * per_slot + index
            copies[at].wait()
            words = words | packed_bits(held.at[at], index * (rows // WORDS))
        bits_ref[place] = jnp.where(live[0, slot] == 1, words, 0)


def stream_kernel(z_ref, self_ref, e2_ref, live_ref, total_ref, bits_ref, held, acc, live, sems):
    rows = held.shape[1]
    cols = z_ref.shape[1]
    pieces = cols // rows
    sources = [slot * pieces + index for slot in (0, 2) for index in range(pieces)]
    copies = [
        pltpu.make_async_copy(e2_ref.at[pl.ds(source * rows, rows)], held.at[index], sems.at[index])
        for index, source in enumerate(sources)
    ]
    copies.append(pltpu.make_async_copy(live_ref, live, sems.at[2 * pieces]))
    for copy in copies:
        copy.start()
    acc[...] = jnp.zeros_like(acc)

    def arrived(index):
        pltpu.make_async_copy(e2_ref.at[pl.ds(0, rows)], held.at[index], sems.at[index]).wait()
        return held.at[index]

    @pl.loop(0, pieces)
    def _(index):
        adjacency = arrived(index)[...].astype(jnp.float32).astype(jnp.bfloat16)
        own = z_ref[:, pl.ds(pl.multiple_of(index * rows, rows), rows)]
        acc[...] += jnp.dot(own, adjacency, preferred_element_type=jnp.float32)

    total_ref[...] = self_ref[...] + acc[...] / FAN2
    bits_ref[...] = jnp.zeros_like(bits_ref)

    @pl.loop(pieces, 2 * pieces)
    def _(index):
        first_bit = (index - pieces) * (rows // WORDS)
        bits_ref[...] = bits_ref[...] | packed_bits(arrived(index), first_bit)

    copies[-1].wait()
    bits_ref[...] = jnp.where(live[0, 2] == 1, bits_ref[...], 0)


def first_kernel(
    hid, depth, p0_ref, p2_ref, p3_ref, p1_ref, e_ref, after_ref, self_ref, z_ref, send_ref, own_ref, x, w1, w2
):
    me = lax.axis_index("feat")
    height = p0_ref.shape[0]
    cols = x.shape[1]
    feats = x.shape[0] // height
    padded = z_ref.shape[0]
    for step, ref in enumerate((p0_ref, p1_ref, p2_ref, p3_ref)):
        place = lax.rem(me + step, feats)
        rows = pl.ds(pl.multiple_of(place * height, height), height)
        x[rows, :] = ref[:, :cols]
        w1[rows, :] = ref[:, cols : cols + hid]
        below = pl.ds(pl.multiple_of((feats + place) * height, height), height)
        w1[below, :] = ref[:, cols + hid : cols + 2 * hid]
        for piece in range(depth // height):
            units = pl.ds(pl.multiple_of(place * depth + piece * height, height), height)
            lanes = slice(cols + 2 * hid + piece * LANES, cols + 2 * hid + (piece + 1) * LANES)
            w2[units, :] = ref[:, lanes]
    inputs = x[...]
    weights = w1[...].astype(jnp.float32).T.astype(jnp.bfloat16)
    project = w2[...].astype(jnp.float32).T.astype(jnp.bfloat16)
    group = lax.broadcasted_iota(jnp.int32, (1, cols), 1) // WORDS
    scale = jnp.ones((1, cols), jnp.float32)
    for bit in range(5):
        scale = scale * jnp.where((group >> bit) % 2 == 1, 2.0 ** -(1 << bit), 1.0)
    scale = jnp.where(group == 31, -scale, scale)
    chunk = 256
    for first in range(0, cols, chunk):
        part = slice(first, first + chunk)
        nbr = jnp.dot(inputs, e_ref[:, part], preferred_element_type=jnp.float32) / FAN1
        stacked = jnp.concatenate([inputs[:, part], nbr.astype(jnp.bfloat16)], axis=0)
        before = jnp.dot(weights, stacked, preferred_element_type=jnp.float32)
        hidden = jnp.maximum(before, 0.0).astype(jnp.bfloat16)
        both = jnp.dot(project, hidden, preferred_element_type=jnp.float32)
        self_ref[:, part] = both[:padded]
        z = both[LANES // 2 : LANES // 2 + padded]
        own_ref[:, part] = z.astype(jnp.bfloat16)
        scaled = (z * scale[:, part]).astype(jnp.bfloat16)
        z_ref[:, part] = scaled
        send_ref[:, part] = scaled


def second_kernel(
    classes, z2_ref, z1_ref, z3_hbm, total_ref, b13_ref, b2_ref, label_ref, loss_ref, sum_ref, z3_ref, acc, sem
):
    padded, cols = total_ref.shape
    fetch = pltpu.make_async_copy(z3_hbm, z3_ref, sem)
    fetch.start()
    chunk = 256

    def edges(words):
        planes = []
        for bit in range(32):
            mask = (1 << bit) if bit < 31 else -(1 << 31)
            planes.append((words & jnp.int32(mask)).astype(jnp.float32).astype(jnp.bfloat16))
        return jnp.concatenate(planes, axis=0)

    for first in range(0, cols, chunk):
        part = slice(first, first + chunk)
        term = jnp.dot(z1_ref[...], edges(b13_ref[0, :, part]), preferred_element_type=jnp.float32)
        acc[:, part] = term + jnp.dot(
            z2_ref[...], edges(b2_ref[:, part]), preferred_element_type=jnp.float32
        )
    fetch.wait()
    class_ids = lax.broadcasted_iota(jnp.int32, (padded, chunk), 0)
    summed = jnp.zeros((1, chunk), jnp.float32)
    for first in range(0, cols, chunk):
        part = slice(first, first + chunk)
        term = acc[:, part] + jnp.dot(
            z3_ref[...], edges(b13_ref[1, :, part]), preferred_element_type=jnp.float32
        )
        logits = total_ref[:, part] + term / FAN2
        powers = jnp.where(class_ids < classes, jnp.exp(logits), 0.0)
        picked = jnp.where(class_ids == label_ref[:, part], logits, 0.0)
        loss = jnp.log(jnp.sum(powers, 0, keepdims=True)) - jnp.sum(picked, 0, keepdims=True)
        loss_ref[:, part] = loss
        summed = summed + loss
    mean = jnp.sum(summed, keepdims=True) / (cols * sum_ref.shape[0])
    sum_ref[...] = jnp.broadcast_to(mean.reshape(1, 1, 1), sum_ref.shape)


def final_kernel(loss_ref, parts_ref, out_ref, mean_ref):
    out_ref[...] = loss_ref[...]
    mean_ref[0, 0] = jnp.sum(parts_ref[:, :, 0:1])


def local(
    features,
    edges_one,
    w1_self,
    w1_nbr,
    need_blocks,
    live_slots,
    edges_two,
    w2_self,
    w2_nbr,
    labels,
):
    rows, block_len = features.shape
    hid = w1_self.shape[1]
    depth, classes = w2_self.shape
    nodes = lax.axis_size("node")
    feats = lax.axis_size("feat")
    height = pl.cdiv(rows, 8) * 8
    width = block_len + 2 * hid + depth // height * LANES
    padded = pl.cdiv(classes, 16) * 16

    packed, early = pl.pallas_call(
        pack_kernel,
        out_shape=(
            jax.ShapeDtypeStruct((height, width), jnp.bfloat16),
            jax.ShapeDtypeStruct((block_len // 2, block_len), jnp.int32),
        ),
        in_specs=[HBM] * 6,
        out_specs=(VMEM, VMEM),
        scratch_shapes=[
            pltpu.VMEM((rows, block_len), jnp.bfloat16),
            pltpu.VMEM((rows, hid), jnp.bfloat16),
            pltpu.VMEM((rows, hid), jnp.bfloat16),
            pltpu.VMEM((classes, depth), jnp.bfloat16),
            pltpu.VMEM((classes, depth), jnp.bfloat16),
            pltpu.VMEM((height, block_len + 2 * hid), jnp.float32),
            pltpu.VMEM((LANES, LANES), jnp.float32),
            pltpu.SemaphoreType.DMA((6,)),
        ],
        compiler_params=pltpu.CompilerParams(vmem_limit_bytes=4 * MIB),
        cost_estimate=pl.CostEstimate(flops=2 * MIB, bytes_accessed=2 * MIB, transcendentals=0),
        name="pack",
    )(*map(in_hbm, (features, w1_self, w1_nbr, w2_self.T, w2_nbr.T, edges_one)))

    blocks = [packed] + [from_ahead(packed, "feat", step) for step in (2, 3, 1)]
    words = block_len // 32
    adjacency, bits_outer, number = pl.pallas_call(
        functools.partial(load_kernel, nodes),
        out_shape=(
            jax.ShapeDtypeStruct(edges_one.shape, jnp.bfloat16),
            jax.ShapeDtypeStruct((2, words, block_len), jnp.int32),
            jax.ShapeDtypeStruct((1,), jnp.int32),
        ),
        in_specs=[HBM, VMEM, HBM, HBM, HBM],
        out_specs=(VMEM, VMEM, SMEM),
        scratch_shapes=[
            pltpu.SMEM(need_blocks.shape, jnp.int32),
            pltpu.SMEM(live_slots.shape, jnp.int32),
            pltpu.VMEM((10, block_len // 4, block_len), jnp.int32),
            pltpu.SemaphoreType.DMA((12,)),
        ],
        compiler_params=pltpu.CompilerParams(vmem_limit_bytes=16 * MIB),
        cost_estimate=pl.CostEstimate(flops=100 * MIB, bytes_accessed=10 * MIB, transcendentals=0),
        name="load",
    )(in_hbm(edges_one), early, *map(in_hbm, (edges_two, need_blocks, live_slots)))
    taken = (0, nodes // 2, nodes - 1)
    steps = [step for step in range(nodes) if step not in taken]
    number = lax.clamp(0, number[0], len(steps) - 1)

    self_term, mine, send, own = pl.pallas_call(
        functools.partial(first_kernel, hid, depth),
        out_shape=(
            jax.ShapeDtypeStruct((padded, block_len), jnp.float32),
            jax.ShapeDtypeStruct((padded, block_len), jnp.bfloat16),
            jax.ShapeDtypeStruct((padded, block_len), jnp.bfloat16),
            jax.ShapeDtypeStruct((padded, block_len), jnp.bfloat16),
        ),
        in_specs=[VMEM] * 5 + [HBM],
        out_specs=(VMEM,) * 4,
        scratch_shapes=[
            pltpu.VMEM((feats * height, block_len), jnp.bfloat16),
            pltpu.VMEM((2 * feats * height, hid), jnp.bfloat16),
            pltpu.VMEM((feats * depth, LANES), jnp.bfloat16),
        ],
        compiler_params=pltpu.CompilerParams(vmem_limit_bytes=16 * MIB),
        cost_estimate=pl.CostEstimate(
            flops=2 * 128 * block_len * block_len, bytes_accessed=4 * MIB, transcendentals=0
        ),
        name="first",
    )(*blocks, adjacency, in_hbm(number[None]))

    behind = from_ahead(mine, "node", nodes - 1)
    half = from_ahead(mine, "node", nodes // 2)

    def with_offset(step, send, own, self_term, edges_two, live_slots):
        fourth = from_ahead(send, "node", step)
        total, bits_two = pl.pallas_call(
            stream_kernel,
            out_shape=(
                jax.ShapeDtypeStruct((padded, block_len), jnp.float32),
                jax.ShapeDtypeStruct((words, block_len), jnp.int32),
            ),
            in_specs=[VMEM, VMEM, HBM, HBM],
            out_specs=(VMEM, VMEM),
            scratch_shapes=[
                pltpu.VMEM((8, block_len // 4, block_len), jnp.int32),
                pltpu.VMEM((padded, block_len), jnp.float32),
                pltpu.SMEM(live_slots.shape, jnp.int32),
                pltpu.SemaphoreType.DMA((9,)),
            ],
            compiler_params=pltpu.CompilerParams(vmem_limit_bytes=12 * MIB),
            cost_estimate=pl.CostEstimate(
                flops=100 * MIB, bytes_accessed=8 * MIB, transcendentals=0
            ),
            name="stream",
        )(own, self_term, in_hbm(edges_two), in_hbm(live_slots))
        return fourth, total, bits_two

    fourth, total, bits_two = lax.switch(
        number,
        [functools.partial(with_offset, step) for step in steps],
        send,
        own,
        self_term,
        edges_two,
        live_slots,
    )

    loss, sums = pl.pallas_call(
        functools.partial(second_kernel, classes),
        out_shape=(
            jax.ShapeDtypeStruct((1, block_len), jnp.float32),
            jax.ShapeDtypeStruct((nodes, 1, LANES), jnp.float32),
        ),
        in_specs=[VMEM, VMEM, HBM] + [VMEM] * 4,
        out_specs=(VMEM, VMEM),
        scratch_shapes=[
            pltpu.VMEM((padded, block_len), jnp.bfloat16),
            pltpu.VMEM((padded, block_len), jnp.float32),
            pltpu.SemaphoreType.DMA,
        ],
        compiler_params=pltpu.CompilerParams(vmem_limit_bytes=16 * MIB),
        cost_estimate=pl.CostEstimate(
            flops=2 * 64 * 3 * block_len * block_len,
            bytes_accessed=2 * MIB,
            transcendentals=padded * block_len,
        ),
        name="second",
    )(behind, half, in_hbm(fourth), total, bits_outer, bits_two, labels[None, :])

    everyone = lax.all_to_all(sums, "node", 0, 0, tiled=True)
    node_loss, mean_loss = pl.pallas_call(
        final_kernel,
        out_shape=(
            jax.ShapeDtypeStruct((1, block_len), jnp.float32),
            jax.ShapeDtypeStruct((1, 1), jnp.float32),
        ),
        in_specs=[VMEM, VMEM],
        out_specs=(VMEM, SMEM),
        compiler_params=pltpu.CompilerParams(vmem_limit_bytes=1 * MIB),
        name="final",
    )(loss, everyone)
    return (node_loss[0], mean_loss[0, 0])


def solution(mesh):
    return jax.shard_map(
        local,
        mesh=mesh,
        in_specs=(
            P("feat", "node"),
            P(None, "node"),
            P("feat", None),
            P("feat", None),
            P("node", None),
            P("node", None),
            P(None, "node"),
            P("feat", None),
            P("feat", None),
            P("node"),
        ),
        out_specs=(P("node"), P()),
        check_vma=False,
    )
```

time: 45.2 us -> 45.1 us (level)
  starting transfers between devices: 12.7 us -> 14.2 us
  Pallas kernels: 15.1 us -> 14.3 us
  other arithmetic: 0.63 us -> 0 us
    pallas_call x1, Pallas kernels: 4.52 us -> 1.63 us  [local(): pl.pallas_call(functools.partial(second_kernel, classes), out_shape=(jax....]
    pallas_call x2 -> x3, Pallas kernels: 5.02 us -> 7.05 us  [the longest x1 4.63 us: local(): pl.pallas_call(functools.partial(load_kernel, nodes), out_shape=(jax.Shap...]
    ppermute x6, starting transfers between devices: 12.7 us -> 14.2 us  [from_ahead(): return lax.ppermute(value, axis, pairs)]
    reduce_sum x1 -> x0, other arithmetic: 0.63 us -> none  [local(): mean_loss = jnp.sum(everyone[:, 0, 0])]
  transfers between devices with their start and end apart: 6 -> 6, of which waited for: 1 -> 1; matrix products, arithmetic and copies ran while one was open for 0% -> 0% of each run, Pallas kernels for 16% -> 18%
where the time goes in v2:
time: 45.1 us; the launch traced here: 44.6 us
  Pallas kernels  14.3 us (32%)
  starting transfers between devices  14.2 us (31%)
  blocking collectives  14 us (31%)
  between operations  1.5 us (3%)
  waiting for transfers between devices  0.47 us (1%)
    ppermute x6, starting transfers between devices, from_ahead(): return lax.ppermute(value, axis, pairs)  14.2 us
    all_to_all x1, blocking collectives, local(): everyone = lax.all_to_all(sums, 'node', 0, 0, tiled=True)  14 us
    pallas_call x1, Pallas kernels, local(): pl.pallas_call(functools.partial(load_kernel, nodes), out_shape=(jax.Shap...  4.63 us
    pallas_call x1, Pallas kernels, with_offset(): pl.pallas_call(stream_kernel, out_shape=(jax.ShapeDtypeStruct((padded, bl...  3.59 us
    pallas_call x1, Pallas kernels, local(): pl.pallas_call(functools.partial(first_kernel, hid, depth), out_shape=(ja...  2.05 us
    pallas_call x1, Pallas kernels, local(): pl.pallas_call(pack_kernel, out_shape=(jax.ShapeDtypeStruct((height, widt...  1.75 us
    pallas_call x1, Pallas kernels, local(): pl.pallas_call(functools.partial(second_kernel, classes), out_shape=(jax....  1.63 us
  transfers between devices with their start and end apart: 6, of which 1 were waited for; matrix products, arithmetic and copies ran while one was open for 0% of the time, Pallas kernels for 18%

profile of v2, /device:TPU:1, one launch (start us, length us, event | category | flops | bytes accessed | tf_op | source)
XLA Modules:
  0.0 44.6 jit_solution(5662774864004797568)
XLA Ops:
  0.6 1.8 %pack.1 = (bf16[32,1792]{1,0:T(8,128)(2,1)S(1)}, s32[512,1024]{1,0:T(8,128)S(1)}) custom-call(bf16[25,1024]{1,0:T(8,128)(2,1)} %refs_0_.1, bf16[25,256]{1,0:T(8,128)(2,1)} %refs_1_.1, bf16[25,256]{1,0:T(8,128)(2,1)} %refs_2_.1, bf16[47,64]{1,0:T(8,128)(2,1)} %bitcast.7, bf16[47,64]{1,0:T(8,128)(2,1)} %bitcast.8, s32[1024,1024]{1,0:T(8,128)} %e1_ref.1), custom_call_target="tpu_custom_call" | custom-call | flops 2097152 | bytes 2097152 | tf_op jit(solution)/shard_map/pack/pallas_call | solution.py:255
  2.4 3.8 %collective-permute-start.29 = (bf16[32,1792]{1,0:T(8,128)(2,1)S(1)}, bf16[32,1792]{1,0:T(8,128)(2,1)S(1)}, u32[]{:S(2)}, u32[]{:S(2)}) collective-permute-start(bf16[32,1792]{1,0:T(8,128)(2,1)S(1)} %get-tuple-element.511.p0_ref), channel_id=1, source_target_pairs={{0,2},{1,3},{2,0},{3,1},{4,6},{5,7},{6,4},{7,5},{8,10},{9,11},{10,... | collective-permute-start | bytes 344072 | tf_op jit(solution)/shard_map/ppermute | solution.py:28
  6.2 0.4 collective-permute-start.30
  6.6 2.3 %collective-permute-start.31 = (bf16[32,1792]{1,0:T(8,128)(2,1)S(1)}, bf16[32,1792]{1,0:T(8,128)(2,1)S(1)}, u32[]{:S(2)}, u32[]{:S(2)}) collective-permute-start(bf16[32,1792]{1,0:T(8,128)(2,1)S(1)} %get-tuple-element.511.p0_ref), channel_id=1, source_target_pairs={{0,3},{1,0},{2,1},{3,2},{4,7},{5,4},{6,5},{7,6},{8,11},{9,8},{10,9... | collective-permute-start | bytes 344072 | tf_op jit(solution)/shard_map/ppermute | solution.py:28
  8.9 4.6 %load.1 = (bf16[1024,1024]{1,0:T(8,128)(2,1)S(1)}, s32[2,32,1024]{2,1,0:T(8,128)S(1)}, s32[1]{0:T(128)}) custom-call(s32[1024,1024]{1,0:T(8,128)} %e1_ref.1, s32[512,1024]{1,0:T(8,128)S(1)} %get-tuple-element.512.ready_ref, s32[4096,1024]{1,0:T(8,128)} %e2_ref.1, s32[1,4]{1,0:T(1,128)} %need_ref.1, s32[1,4]{1,0:T(1,128)} %live_ref.1), custom_call_target="tpu_custom_call" | custom-call | flops 104857600 | bytes 10485760 | tf_op jit(solution)/shard_map/load/pallas_call | solution.py:280
  14.2 0.0 collective-permute-done.29.p2_ref
  14.2 0.0 collective-permute-done.30.p3_ref
  14.2 0.0 collective-permute-done.31.p1_ref
  14.2 2.1 %first.1 = (f32[48,1024]{1,0:T(8,128)S(1)}, bf16[48,1024]{1,0:T(8,128)(2,1)S(1)}, bf16[48,1024]{1,0:T(8,128)(2,1)S(1)}, bf16[48,1024]{1,0:T(8,128)(2,1)S(1)}) custom-call(bf16[32,1792]{1,0:T(8,128)(2,1)S(1)} %get-tuple-element.511.p0_ref, bf16[32,1792]{1,0:T(8,128)(2,1)S(1)} %collective-permute-done.29.p2_ref, ...), custom_call_target="tpu_custom_call" | custom-call | flops 268435456 | bytes 4194304 | tf_op jit(solution)/shard_map/first/pallas_call | solution.py:303
  16.3 3.1 %collective-permute-start.32 = (bf16[48,1024]{1,0:T(8,128)(2,1)S(1)}, bf16[48,1024]{1,0:T(8,128)(2,1)S(1)}, u32[]{:S(2)}, u32[]{:S(2)}) collective-permute-start(bf16[48,1024]{1,0:T(8,128)(2,1)S(1)} %get-tuple-element.515), channel_id=1, source_target_pairs={{0,4},{4,8},{8,12},{12,16},{16,20},{20,24},{24,28},{28,32},{32,36}... | collective-permute-start | bytes 294920 | tf_op jit(solution)/shard_map/ppermute | solution.py:28
  19.4 2.7 %collective-permute-start.33 = (bf16[48,1024]{1,0:T(8,128)(2,1)S(1)}, bf16[48,1024]{1,0:T(8,128)(2,1)S(1)}, u32[]{:S(2)}, u32[]{:S(2)}) collective-permute-start(bf16[48,1024]{1,0:T(8,128)(2,1)S(1)} %get-tuple-element.515), channel_id=1, source_target_pairs={{0,64},{4,68},{8,72},{12,76},{16,80},{20,84},{24,88},{28,92},{32,9... | collective-permute-start | bytes 294920 | tf_op jit(solution)/shard_map/ppermute | solution.py:28
  22.1 0.0 copy-start
  22.1 6.0 %conditional.1 = (bf16[48,1024]{1,0:T(8,128)(2,1)}, f32[48,1024]{1,0:T(8,128)S(1)}, s32[32,1024]{1,0:T(8,128)S(1)}) conditional(s32[]{:T(128)} %bitcast.2, (bf16[48,1024]{1,0:T(8,128)(2,1)S(1)}, bf16[48,1024]{1,0:T(8,128)(2,1)S(1)}, f32[48,1024]{1,0:T(8,128)S(1)}, s32[4096,1024]{1,0:T(8,128)}, ...), branch_computations={%region_0.0_spmd, %region_1.0_spmd, %region_2.0_spmd, %region_3.0_... | conditional | flops 104857600 | bytes 8781888 | solution.py:352
  22.1 1.9 %collective-permute-start.9 = (bf16[48,1024]{1,0:T(8,128)(2,1)S(1)}, bf16[48,1024]{1,0:T(8,128)(2,1)}, u32[]{:S(2)}, u32[]{:S(2)}) collective-permute-start(bf16[48,1024]{1,0:T(8,128)(2,1)S(1)} %get-tuple-element.353), channel_id=1, source_target_pairs={{0,88},{4,92},{8,96},{12,100},{16,104},{20,108},{24,112},{28,116},... | collective-permute-start | bytes 294920 | tf_op jit(solution)/shard_map/cond/branch_9_fun/ppermute | solution.py:28
  24.0 3.6 %stream.38 = (f32[48,1024]{1,0:T(8,128)S(1)}, s32[32,1024]{1,0:T(8,128)S(1)}) custom-call(bf16[48,1024]{1,0:T(8,128)(2,1)S(1)} %get-tuple-element.354.z_ref, f32[48,1024]{1,0:T(8,128)S(1)} %get-tuple-element.355.self_ref, s32[4096,1024]{1,0:T(8,128)} %get-tuple-element.356.e2_ref, s32[1,4]{1,0:T(1,128)} %get-tuple-element.357.live_ref), custom_call_target="tpu_custom_call" | custom-call | flops 104857600 | bytes 8388608 | tf_op jit(solution)/shard_map/cond/branch_9_fun/stream/pallas_call | solution.py:330
  27.6 0.5 %collective-permute-done.9 = bf16[48,1024]{1,0:T(8,128)(2,1)} collective-permute-done((bf16[48,1024]{1,0:T(8,128)(2,1)S(1)}, bf16[48,1024]{1,0:T(8,128)(2,1)}, u32[]{:S(2)}, u32[]{:S(2)}) %collective-permute-start.9) | collective-permute-done | bytes 98336 | tf_op jit(solution)/shard_map/cond/branch_9_fun/ppermute | solution.py:28
  28.1 0.0 collective-permute-done.32.z2_ref
  28.1 0.0 collective-permute-done.33.z1_ref
  28.1 0.0 copy-done
  28.1 1.6 %second.1 = (f32[1,1024]{1,0:T(1,128)S(1)}, f32[32,1,128]{2,1,0:T(1,128)S(1)}) custom-call(bf16[48,1024]{1,0:T(8,128)(2,1)S(1)} %collective-permute-done.32.z2_ref, bf16[48,1024]{1,0:T(8,128)(2,1)S(1)} %collective-permute-done.33.z1_ref, bf16[48,1024]{1,0:T(8,128)(2,1)} %get-tuple-element.519.z3_hbm, f32[48,1024]{1,0:T(8,128)S(1)} %get-tuple-element.520.total_ref, ...), custom_call_target="tpu_custom_call" | custom-call | flops 402653184 | bytes 2097152 | tf_op jit(solution)/shard_map/second/pallas_call | solution.py:362
  29.7 14.0 %all_to_all.5.parts_ref = f32[32,1,128]{2,1,0:T(1,128)S(1)} all-to-all(f32[32,1,128]{2,1,0:T(1,128)S(1)} %get-tuple-element.524), channel_id=1, replica_groups=mesh['node'=32,'feat'=4] {'node'}, dimensions={0} | all-to-all | bytes 32768 | tf_op jit(solution)/shard_map/all_to_all | solution.py:384
  43.8 0.7 %final.1 = (f32[1,1024]{1,0:T(1,128)}, f32[1,1]{1,0:T(1,128)}) custom-call(f32[1,1024]{1,0:T(1,128)S(1)} %get-tuple-element.523.loss_ref, f32[32,1,128]{2,1,0:T(1,128)S(1)} %all_to_all.5.parts_ref), custom_call_target="tpu_custom_call" | custom-call | tf_op jit(solution)/shard_map/final/pallas_call | solution.py:385
Async XLA Ops:
  2.4 11.8 %collective-permute-start.29 = (bf16[32,1792]{1,0:T(8,128)(2,1)S(1)}, bf16[32,1792]{1,0:T(8,128)(2,1)S(1)}, u32[]{:S(2)}, u32[]{:S(2)}) collective-permute-start(bf16[32,1792]{1,0:T(8,128)(2,1)S(1)} %get-tuple-element.511.p0_ref), channel_id=1, source_target_pairs={{0,2},{1,3},{2,0},{3,1},{4,6},{5,7},{6,4},{7,5},{8,10},{9,11},{10,... | collective-permute-start | bytes 344072 | tf_op jit(solution)/shard_map/ppermute | solution.py:28
  6.2 8.0 %collective-permute-start.30 = (bf16[32,1792]{1,0:T(8,128)(2,1)S(1)}, bf16[32,1792]{1,0:T(8,128)(2,1)S(1)}, u32[]{:S(2)}, u32[]{:S(2)}) collective-permute-start(bf16[32,1792]{1,0:T(8,128)(2,1)S(1)} %get-tuple-element.511.p0_ref), channel_id=1, source_target_pairs={{0,1},{1,2},{2,3},{3,0},{4,5},{5,6},{6,7},{7,4},{8,9},{9,10},{10,1... | collective-permute-start | bytes 344072 | tf_op jit(solution)/shard_map/ppermute | solution.py:28
  6.6 7.6 %collective-permute-start.31 = (bf16[32,1792]{1,0:T(8,128)(2,1)S(1)}, bf16[32,1792]{1,0:T(8,128)(2,1)S(1)}, u32[]{:S(2)}, u32[]{:S(2)}) collective-permute-start(bf16[32,1792]{1,0:T(8,128)(2,1)S(1)} %get-tuple-element.511.p0_ref), channel_id=1, source_target_pairs={{0,3},{1,0},{2,1},{3,2},{4,7},{5,4},{6,5},{7,6},{8,11},{9,8},{10,9... | collective-permute-start | bytes 344072 | tf_op jit(solution)/shard_map/ppermute | solution.py:28
  16.3 11.8 %collective-permute-start.32 = (bf16[48,1024]{1,0:T(8,128)(2,1)S(1)}, bf16[48,1024]{1,0:T(8,128)(2,1)S(1)}, u32[]{:S(2)}, u32[]{:S(2)}) collective-permute-start(bf16[48,1024]{1,0:T(8,128)(2,1)S(1)} %get-tuple-element.515), channel_id=1, source_target_pairs={{0,4},{4,8},{8,12},{12,16},{16,20},{20,24},{24,28},{28,32},{32,36}... | collective-permute-start | bytes 294920 | tf_op jit(solution)/shard_map/ppermute | solution.py:28
  19.4 8.7 %collective-permute-start.33 = (bf16[48,1024]{1,0:T(8,128)(2,1)S(1)}, bf16[48,1024]{1,0:T(8,128)(2,1)S(1)}, u32[]{:S(2)}, u32[]{:S(2)}) collective-permute-start(bf16[48,1024]{1,0:T(8,128)(2,1)S(1)} %get-tuple-element.515), channel_id=1, source_target_pairs={{0,64},{4,68},{8,72},{12,76},{16,80},{20,84},{24,88},{28,92},{32,9... | collective-permute-start | bytes 294920 | tf_op jit(solution)/shard_map/ppermute | solution.py:28
  22.1 6.0 %copy-start = (s32[1024]{0:T(1024)S(1)}, s32[1024]{0:T(1024)}, u32[]{:S(2)}) copy-start(s32[1024]{0:T(1024)} %param.48) | copy-start | bytes 12292
  22.1 6.0 %collective-permute-start.9 = (bf16[48,1024]{1,0:T(8,128)(2,1)S(1)}, bf16[48,1024]{1,0:T(8,128)(2,1)}, u32[]{:S(2)}, u32[]{:S(2)}) collective-permute-start(bf16[48,1024]{1,0:T(8,128)(2,1)S(1)} %get-tuple-element.353), channel_id=1, source_target_pairs={{0,88},{4,92},{8,96},{12,100},{16,104},{20,108},{24,112},{28,116},... | collective-permute-start | bytes 294920 | tf_op jit(solution)/shard_map/cond/branch_9_fun/ppermute | solution.py:28

commit v3 on v2

--- a/solution.py
+++ b/solution.py
@@ -11,6 +11,7 @@
 FAN2 = 10
 LANES = 128
 WORDS = 32
+EARLY = 2
 MIB = 1 << 20
 
 VMEM = pl.BlockSpec(memory_space=pltpu.VMEM)
@@ -29,13 +30,11 @@
 
 
 def pack_kernel(*refs):
-    sources, (out_ref, edges_ref), held, (scr, cat, sems) = refs[:6], refs[6:8], refs[8:13], refs[13:]
+    sources, out_ref, held, (scr, cat, sems) = refs[:5], refs[5], refs[6:11], refs[11:]
     copies = [
         pltpu.make_async_copy(source, place, sems.at[index])
-        for index, (source, place) in enumerate(zip(sources[:5], held))
+        for index, (source, place) in enumerate(zip(sources, held))
     ]
-    ahead = sources[5].at[pl.ds(0, edges_ref.shape[0])]
-    copies.append(pltpu.make_async_copy(ahead, edges_ref, sems.at[5]))
     for copy in copies:
         copy.start()
     x_ref, ws_ref, wn_ref, us_ref, un_ref = held
@@ -46,7 +45,7 @@
     side = cols + 2 * hid
     scr[rows:, :] = jnp.zeros((height - rows, side), jnp.float32)
     cat[...] = jnp.zeros_like(cat)
-    for copy in copies[:5]:
+    for copy in copies:
         copy.wait()
     scr[:rows, :cols] = x_ref[...].astype(jnp.float32)
     scr[:rows, cols : cols + hid] = ws_ref[...].astype(jnp.float32)
@@ -58,7 +57,6 @@
     for piece in range(depth // height):
         place = slice(side + piece * LANES, side + (piece + 1) * LANES)
         out_ref[:, place] = by_unit[piece * height : (piece + 1) * height].astype(jnp.bfloat16)
-    copies[5].wait()
 
 
 def packed_bits(piece, first_bit):
@@ -69,16 +67,25 @@
     return words
 
 
+def pack_slot(pieces, first_bit):
+    words = None
+    for index, arrived in enumerate(pieces):
+        piece = arrived()
+        bits = packed_bits(piece, first_bit + index * (piece.shape[0] // WORDS))
+        words = bits if words is None else words | bits
+    return words
+
+
 def load_kernel(
-    nodes, e1_ref, ready_ref, e2_ref, need_ref, live_ref, e1_out, bits_ref, number_ref, need, live, held, sems
+    nodes, e1_ref, e2_ref, need_ref, live_ref, after_ref, e1_out, bits_ref, number_ref, need, live, held, sems
 ):
-    pieces, rows = bits_ref.shape[0] * 4, held.shape[1]
+    rows = held.shape[1]
     cols = e1_out.shape[0]
-    done = ready_ref.shape[0]
-    sources = [e1_ref.at[pl.ds(first, rows)] for first in range(done, cols, rows)]
-    before = len(sources)
-    for slot in (1, 3):
-        sources += [e2_ref.at[pl.ds(first, rows)] for first in range(slot * cols, (slot + 1) * cols, rows)]
+    per_slot = cols // rows
+    extra = held.shape[0] - 2 * per_slot
+    sources = [e1_ref.at[pl.ds(index * rows, rows)] for index in range(per_slot)]
+    sources += [e2_ref.at[pl.ds(cols + index * rows, rows)] for index in range(per_slot)]
+    sources += [e2_ref.at[pl.ds(3 * cols + index * rows, rows)] for index in range(extra)]
     copies = [
         pltpu.make_async_copy(source, held.at[index], sems.at[index])
         for index, source in enumerate(sources)
@@ -89,35 +96,35 @@
     ]
     for copy in small + copies:
         copy.start()
-    e1_out[:done, :] = ready_ref[...].astype(jnp.float32).astype(jnp.bfloat16)
     for copy in small:
         copy.wait()
     offset = lax.rem(need[0, 3] - lax.axis_index("node") + nodes, nodes)
     number_ref[0] = offset - 1 - (offset > nodes // 2).astype(jnp.int32)
-    for index in range(before):
+
+    def arrived(index):
         copies[index].wait()
-        first = done + index * rows
-        e1_out[first : first + rows, :] = held[index].astype(jnp.float32).astype(jnp.bfloat16)
-    per_slot = cols // rows
-    for place, slot in enumerate((1, 3)):
-        words = jnp.zeros(bits_ref.shape[1:], jnp.int32)
-        for index in range(per_slot):
-            at = before + place * per_slot + index
-            copies[at].wait()
-            words = words | packed_bits(held.at[at], index * (rows // WORDS))
-        bits_ref[place] = jnp.where(live[0, slot] == 1, words, 0)
+        return held.at[index]
+
+    for index in range(per_slot):
+        piece = arrived(index)[...].astype(jnp.float32).astype(jnp.bfloat16)
+        e1_out[index * rows : (index + 1) * rows, :] = piece
+    for place, slot, begin, count in ((0, 1, per_slot, per_slot), (1, 3, 2 * per_slot, extra)):
+        pieces = [functools.partial(arrived, begin + index) for index in range(count)]
+        bits_ref[place] = jnp.where(live[0, slot] == 1, pack_slot(pieces, 0), 0)
 
 
 def stream_kernel(z_ref, self_ref, e2_ref, live_ref, total_ref, bits_ref, held, acc, live, sems):
     rows = held.shape[1]
     cols = z_ref.shape[1]
     pieces = cols // rows
+    late = held.shape[0] - 2 * pieces
     sources = [slot * pieces + index for slot in (0, 2) for index in range(pieces)]
+    sources += [4 * pieces - late + index for index in range(late)]
     copies = [
         pltpu.make_async_copy(e2_ref.at[pl.ds(source * rows, rows)], held.at[index], sems.at[index])
         for index, source in enumerate(sources)
     ]
-    copies.append(pltpu.make_async_copy(live_ref, live, sems.at[2 * pieces]))
+    copies.append(pltpu.make_async_copy(live_ref, live, sems.at[len(sources)]))
     for copy in copies:
         copy.start()
     acc[...] = jnp.zeros_like(acc)
@@ -135,13 +142,16 @@
     total_ref[...] = self_ref[...] + acc[...] / FAN2
     bits_ref[...] = jnp.zeros_like(bits_ref)
 
-    @pl.loop(pieces, 2 * pieces)
-    def _(index):
-        first_bit = (index - pieces) * (rows // WORDS)
-        bits_ref[...] = bits_ref[...] | packed_bits(arrived(index), first_bit)
+    for place, begin, count in ((0, pieces, pieces), (1, 2 * pieces, late)):
+
+        @pl.loop(0, count)
+        def _(index):
+            first_bit = (index + pieces - count) * (rows // WORDS)
+            bits_ref[place] = bits_ref[place] | packed_bits(arrived(begin + index), first_bit)
 
     copies[-1].wait()
-    bits_ref[...] = jnp.where(live[0, 2] == 1, bits_ref[...], 0)
+    for place, slot in enumerate((2, 3)):
+        bits_ref[place] = jnp.where(live[0, slot] == 1, bits_ref[place], 0)
 
 
 def first_kernel(
@@ -171,24 +181,21 @@
     for bit in range(5):
         scale = scale * jnp.where((group >> bit) % 2 == 1, 2.0 ** -(1 << bit), 1.0)
     scale = jnp.where(group == 31, -scale, scale)
-    chunk = 256
-    for first in range(0, cols, chunk):
-        part = slice(first, first + chunk)
-        nbr = jnp.dot(inputs, e_ref[:, part], preferred_element_type=jnp.float32) / FAN1
-        stacked = jnp.concatenate([inputs[:, part], nbr.astype(jnp.bfloat16)], axis=0)
-        before = jnp.dot(weights, stacked, preferred_element_type=jnp.float32)
-        hidden = jnp.maximum(before, 0.0).astype(jnp.bfloat16)
-        both = jnp.dot(project, hidden, preferred_element_type=jnp.float32)
-        self_ref[:, part] = both[:padded]
-        z = both[LANES // 2 : LANES // 2 + padded]
-        own_ref[:, part] = z.astype(jnp.bfloat16)
-        scaled = (z * scale[:, part]).astype(jnp.bfloat16)
-        z_ref[:, part] = scaled
-        send_ref[:, part] = scaled
+    nbr = jnp.dot(inputs, e_ref[...], preferred_element_type=jnp.float32) / FAN1
+    stacked = jnp.concatenate([inputs, nbr.astype(jnp.bfloat16)], axis=0)
+    before = jnp.dot(weights, stacked, preferred_element_type=jnp.float32)
+    hidden = jnp.maximum(before, 0.0).astype(jnp.bfloat16)
+    both = jnp.dot(project, hidden, preferred_element_type=jnp.float32)
+    self_ref[...] = both[:padded]
+    z = both[LANES // 2 : LANES // 2 + padded]
+    own_ref[...] = z.astype(jnp.bfloat16)
+    scaled = (z * scale).astype(jnp.bfloat16)
+    z_ref[...] = scaled
+    send_ref[...] = scaled
 
 
 def second_kernel(
-    classes, z2_ref, z1_ref, z3_hbm, total_ref, b13_ref, b2_ref, label_ref, loss_ref, sum_ref, z3_ref, acc, sem
+    classes, z2_ref, z1_ref, z3_hbm, total_ref, b13_ref, b23_ref, label_ref, loss_ref, sum_ref, z3_ref, acc, sem
 ):
     padded, cols = total_ref.shape
     fetch = pltpu.make_async_copy(z3_hbm, z3_ref, sem)
@@ -206,7 +213,7 @@
         part = slice(first, first + chunk)
         term = jnp.dot(z1_ref[...], edges(b13_ref[0, :, part]), preferred_element_type=jnp.float32)
         acc[:, part] = term + jnp.dot(
-            z2_ref[...], edges(b2_ref[:, part]), preferred_element_type=jnp.float32
+            z2_ref[...], edges(b23_ref[0, :, part]), preferred_element_type=jnp.float32
         )
     fetch.wait()
     class_ids = lax.broadcasted_iota(jnp.int32, (padded, chunk), 0)
@@ -214,7 +221,8 @@
     for first in range(0, cols, chunk):
         part = slice(first, first + chunk)
         term = acc[:, part] + jnp.dot(
-            z3_ref[...], edges(b13_ref[1, :, part]), preferred_element_type=jnp.float32
+            z3_ref[...],
+            edges(b13_ref[1, :, part] | b23_ref[1, :, part]), preferred_element_type=jnp.float32
         )
         logits = total_ref[:, part] + term / FAN2
         powers = jnp.where(class_ids < classes, jnp.exp(logits), 0.0)
@@ -252,14 +260,11 @@
     width = block_len + 2 * hid + depth // height * LANES
     padded = pl.cdiv(classes, 16) * 16
 
-    packed, early = pl.pallas_call(
+    packed = pl.pallas_call(
         pack_kernel,
-        out_shape=(
-            jax.ShapeDtypeStruct((height, width), jnp.bfloat16),
-            jax.ShapeDtypeStruct((block_len // 2, block_len), jnp.int32),
-        ),
-        in_specs=[HBM] * 6,
-        out_specs=(VMEM, VMEM),
+        out_shape=jax.ShapeDtypeStruct((height, width), jnp.bfloat16),
+        in_specs=[HBM] * 5,
+        out_specs=VMEM,
         scratch_shapes=[
             pltpu.VMEM((rows, block_len), jnp.bfloat16),
             pltpu.VMEM((rows, hid), jnp.bfloat16),
@@ -268,12 +273,12 @@
             pltpu.VMEM((classes, depth), jnp.bfloat16),
             pltpu.VMEM((height, block_len + 2 * hid), jnp.float32),
             pltpu.VMEM((LANES, LANES), jnp.float32),
-            pltpu.SemaphoreType.DMA((6,)),
+            pltpu.SemaphoreType.DMA((5,)),
         ],
         compiler_params=pltpu.CompilerParams(vmem_limit_bytes=4 * MIB),
-        cost_estimate=pl.CostEstimate(flops=2 * MIB, bytes_accessed=2 * MIB, transcendentals=0),
+        cost_estimate=pl.CostEstimate(flops=2 * MIB, bytes_accessed=MIB // 4, transcendentals=0),
         name="pack",
-    )(*map(in_hbm, (features, w1_self, w1_nbr, w2_self.T, w2_nbr.T, edges_one)))
+    )(*map(in_hbm, (features, w1_self, w1_nbr, w2_self.T, w2_nbr.T)))
 
     blocks = [packed] + [from_ahead(packed, "feat", step) for step in (2, 3, 1)]
     words = block_len // 32
@@ -284,18 +289,18 @@
             jax.ShapeDtypeStruct((2, words, block_len), jnp.int32),
             jax.ShapeDtypeStruct((1,), jnp.int32),
         ),
-        in_specs=[HBM, VMEM, HBM, HBM, HBM],
+        in_specs=[HBM] * 4 + [VMEM],
         out_specs=(VMEM, VMEM, SMEM),
         scratch_shapes=[
             pltpu.SMEM(need_blocks.shape, jnp.int32),
             pltpu.SMEM(live_slots.shape, jnp.int32),
-            pltpu.VMEM((10, block_len // 4, block_len), jnp.int32),
-            pltpu.SemaphoreType.DMA((12,)),
+            pltpu.VMEM((8 + EARLY, block_len // 4, block_len), jnp.int32),
+            pltpu.SemaphoreType.DMA((10 + EARLY,)),
         ],
         compiler_params=pltpu.CompilerParams(vmem_limit_bytes=16 * MIB),
         cost_estimate=pl.CostEstimate(flops=100 * MIB, bytes_accessed=10 * MIB, transcendentals=0),
         name="load",
-    )(in_hbm(edges_one), early, *map(in_hbm, (edges_two, need_blocks, live_slots)))
+    )(*map(in_hbm, (edges_one, edges_two, need_blocks, live_slots)), packed)
     taken = (0, nodes // 2, nodes - 1)
     steps = [step for step in range(nodes) if step not in taken]
     number = lax.clamp(0, number[0], len(steps) - 1)
@@ -331,17 +336,17 @@
             stream_kernel,
             out_shape=(
                 jax.ShapeDtypeStruct((padded, block_len), jnp.float32),
-                jax.ShapeDtypeStruct((words, block_len), jnp.int32),
+                jax.ShapeDtypeStruct((2, words, block_len), jnp.int32),
             ),
             in_specs=[VMEM, VMEM, HBM, HBM],
             out_specs=(VMEM, VMEM),
             scratch_shapes=[
-                pltpu.VMEM((8, block_len // 4, block_len), jnp.int32),
+                pltpu.VMEM((12 - EARLY, block_len // 4, block_len), jnp.int32),
                 pltpu.VMEM((padded, block_len), jnp.float32),
                 pltpu.SMEM(live_slots.shape, jnp.int32),
-                pltpu.SemaphoreType.DMA((9,)),
+                pltpu.SemaphoreType.DMA((13 - EARLY,)),
             ],
-            compiler_params=pltpu.CompilerParams(vmem_limit_bytes=12 * MIB),
+            compiler_params=pltpu.CompilerParams(vmem_limit_bytes=16 * MIB),
             cost_estimate=pl.CostEstimate(
                 flops=100 * MIB, bytes_accessed=8 * MIB, transcendentals=0
             ),

time: 45.1 us -> 42.3 us (0.938)
  blocking collectives: 14 us -> 12.4 us
  Pallas kernels: 14.3 us -> 13 us
  starting transfers between devices: 14.2 us -> 13.3 us
  waiting for transfers between devices: 0.47 us -> 1.32 us
    all_to_all x1, blocking collectives: 14 us -> 12.4 us  [local(): everyone = lax.all_to_all(sums, 'node', 0, 0, tiled=True)]
    pallas_call x1, Pallas kernels: 2.05 us -> 0.85 us  [local(): pl.pallas_call(functools.partial(first_kernel, hid, depth), out_shape=(ja...]
    ppermute x6, starting transfers between devices: 14.2 us -> 13.3 us  [from_ahead(): return lax.ppermute(value, axis, pairs)]
    ppermute x6, waiting for transfers between devices: 0.47 us -> 1.32 us  [from_ahead(): return lax.ppermute(value, axis, pairs)]
    pallas_call x1, Pallas kernels: 1.75 us -> 0.99 us  [local(): pl.pallas_call(pack_kernel, out_shape=jax.ShapeDtypeStruct((height, width...]
    pallas_call x1, Pallas kernels: 3.59 us -> 4.22 us  [with_offset(): pl.pallas_call(stream_kernel, out_shape=(jax.ShapeDtypeStruct((padded, bl...]
  transfers between devices with their start and end apart: 6 -> 6, of which waited for: 1 -> 2; matrix products, arithmetic and copies ran while one was open for 0% -> 0% of each run, Pallas kernels for 18% -> 21%
where the time goes in v3:
time: 42.3 us; the launch traced here: 41.5 us
  starting transfers between devices  13.3 us (31%)
  Pallas kernels  13 us (31%)
  blocking collectives  12.4 us (29%)
  between operations  1.49 us (4%)
  waiting for transfers between devices  1.32 us (3%)
    ppermute x6, starting transfers between devices, from_ahead(): return lax.ppermute(value, axis, pairs)  13.3 us
    all_to_all x1, blocking collectives, local(): everyone = lax.all_to_all(sums, 'node', 0, 0, tiled=True)  12.4 us
    pallas_call x1, Pallas kernels, local(): pl.pallas_call(functools.partial(load_kernel, nodes), out_shape=(jax.Shap...  4.63 us
    pallas_call x1, Pallas kernels, with_offset(): pl.pallas_call(stream_kernel, out_shape=(jax.ShapeDtypeStruct((padded, bl...  4.22 us
    pallas_call x1, Pallas kernels, local(): pl.pallas_call(functools.partial(second_kernel, classes), out_shape=(jax....  1.64 us
    ppermute x6, waiting for transfers between devices, from_ahead(): return lax.ppermute(value, axis, pairs)  1.32 us
    pallas_call x1, Pallas kernels, local(): pl.pallas_call(pack_kernel, out_shape=jax.ShapeDtypeStruct((height, width...  0.99 us
    pallas_call x1, Pallas kernels, local(): pl.pallas_call(functools.partial(first_kernel, hid, depth), out_shape=(ja...  0.85 us
  transfers between devices with their start and end apart: 6, of which 2 were waited for; matrix products, arithmetic and copies ran while one was open for 0% of the time, Pallas kernels for 21%

profile of v3, /device:TPU:1, one launch (start us, length us, event | category | flops | bytes accessed | tf_op | source)
XLA Modules:
  0.0 41.5 jit_solution(5952375139683896135)
XLA Ops:
  0.6 1.0 %pack.1.after_ref.p0_ref = bf16[32,1792]{1,0:T(8,128)(2,1)S(1)} custom-call(bf16[25,1024]{1,0:T(8,128)(2,1)} %refs_0_.1, bf16[25,256]{1,0:T(8,128)(2,1)} %refs_1_.1, bf16[25,256]{1,0:T(8,128)(2,1)} %refs_2_.1, bf16[47,64]{1,0:T(8,128)(2,1)} %bitcast.7, bf16[47,64]{1,0:T(8,128)(2,1)} %bitcast.8), custom_call_target="tpu_custom_call" | custom-call | flops 2097152 | bytes 262144 | tf_op jit(solution)/shard_map/pack/pallas_call | solution.py:263
  1.6 3.6 %collective-permute-start.31 = (bf16[32,1792]{1,0:T(8,128)(2,1)S(1)}, bf16[32,1792]{1,0:T(8,128)(2,1)S(1)}, u32[]{:S(2)}, u32[]{:S(2)}) collective-permute-start(bf16[32,1792]{1,0:T(8,128)(2,1)S(1)} %pack.1.after_ref.p0_ref), channel_id=1, source_target_pairs={{0,3},{1,0},{2,1},{3,2},{4,7},{5,4},{6,5},{7,6},{8,11},{9,8},{10,9... | collective-permute-start | bytes 344072 | tf_op jit(solution)/shard_map/ppermute | solution.py:29
  5.3 0.0 collective-permute-start.30
  5.3 1.6 %collective-permute-start.29 = (bf16[32,1792]{1,0:T(8,128)(2,1)S(1)}, bf16[32,1792]{1,0:T(8,128)(2,1)S(1)}, u32[]{:S(2)}, u32[]{:S(2)}) collective-permute-start(bf16[32,1792]{1,0:T(8,128)(2,1)S(1)} %pack.1.after_ref.p0_ref), channel_id=1, source_target_pairs={{0,2},{1,3},{2,0},{3,1},{4,6},{5,7},{6,4},{7,5},{8,10},{9,11},{10,... | collective-permute-start | bytes 344072 | tf_op jit(solution)/shard_map/ppermute | solution.py:29
  6.9 4.6 %load.1 = (bf16[1024,1024]{1,0:T(8,128)(2,1)S(1)}, s32[2,32,1024]{2,1,0:T(8,128)S(1)}, s32[1]{0:T(128)}) custom-call(s32[1024,1024]{1,0:T(8,128)} %e1_ref.1, s32[4096,1024]{1,0:T(8,128)} %e2_ref.1, s32[1,4]{1,0:T(1,128)} %need_ref.1, s32[1,4]{1,0:T(1,128)} %live_ref.1, bf16[32,1792]{1,0:T(8,128)(2,1)S(1)} %pack.1.after_ref.p0_ref), custom_call_target="tpu_custom_call" | custom-call | flops 104857600 | bytes 10485760 | tf_op jit(solution)/shard_map/load/pallas_call | solution.py:285
  12.2 0.0 collective-permute-done.31.p1_ref
  12.2 1.1 %collective-permute-done.30.p3_ref = bf16[32,1792]{1,0:T(8,128)(2,1)S(1)} collective-permute-done((bf16[32,1792]{1,0:T(8,128)(2,1)S(1)}, bf16[32,1792]{1,0:T(8,128)(2,1)S(1)}, u32[]{:S(2)}, u32[]{:S(2)}) %collective-permute-start.30) | collective-permute-done | bytes 114720 | tf_op jit(solution)/shard_map/ppermute | solution.py:29
  13.3 0.0 collective-permute-done.29.p2_ref
  13.3 0.9 %first.1 = (f32[48,1024]{1,0:T(8,128)S(1)}, bf16[48,1024]{1,0:T(8,128)(2,1)S(1)}, bf16[48,1024]{1,0:T(8,128)(2,1)S(1)}, bf16[48,1024]{1,0:T(8,128)(2,1)S(1)}) custom-call(bf16[32,1792]{1,0:T(8,128)(2,1)S(1)} %pack.1.after_ref.p0_ref, bf16[32,1792]{1,0:T(8,128)(2,1)S(1)} %collective-permute-done.29.p2_ref, ...), custom_call_target="tpu_custom_call" | custom-call | flops 268435456 | bytes 4194304 | tf_op jit(solution)/shard_map/first/pallas_call | solution.py:308
  14.1 2.8 %collective-permute-start.33 = (bf16[48,1024]{1,0:T(8,128)(2,1)S(1)}, bf16[48,1024]{1,0:T(8,128)(2,1)S(1)}, u32[]{:S(2)}, u32[]{:S(2)}) collective-permute-start(bf16[48,1024]{1,0:T(8,128)(2,1)S(1)} %get-tuple-element.511), channel_id=1, source_target_pairs={{0,64},{4,68},{8,72},{12,76},{16,80},{20,84},{24,88},{28,92},{32,9... | collective-permute-start | bytes 294920 | tf_op jit(solution)/shard_map/ppermute | solution.py:29
  17.0 3.0 %collective-permute-start.32 = (bf16[48,1024]{1,0:T(8,128)(2,1)S(1)}, bf16[48,1024]{1,0:T(8,128)(2,1)S(1)}, u32[]{:S(2)}, u32[]{:S(2)}) collective-permute-start(bf16[48,1024]{1,0:T(8,128)(2,1)S(1)} %get-tuple-element.511), channel_id=1, source_target_pairs={{0,4},{4,8},{8,12},{12,16},{16,20},{20,24},{24,28},{28,32},{32,36}... | collective-permute-start | bytes 294920 | tf_op jit(solution)/shard_map/ppermute | solution.py:29
  20.0 0.0 copy-start
  20.0 6.7 %conditional.1 = (bf16[48,1024]{1,0:T(8,128)(2,1)}, f32[48,1024]{1,0:T(8,128)S(1)}, s32[2,32,1024]{2,1,0:T(8,128)S(1)}) conditional(s32[]{:T(128)} %bitcast.2, (bf16[48,1024]{1,0:T(8,128)(2,1)S(1)}, bf16[48,1024]{1,0:T(8,128)(2,1)S(1)}, f32[48,1024]{1,0:T(8,128)S(1)}, s32[4096,1024]{1,0:T(8,128)}, ...), branch_computations={%region_0.0_spmd, %region_1.0_spmd, %region_2.0_spmd, %region_3.0_... | conditional | flops 104857600 | bytes 8781888 | solution.py:357
  20.0 2.2 %collective-permute-start.5 = (bf16[48,1024]{1,0:T(8,128)(2,1)S(1)}, bf16[48,1024]{1,0:T(8,128)(2,1)}, u32[]{:S(2)}, u32[]{:S(2)}) collective-permute-start(bf16[48,1024]{1,0:T(8,128)(2,1)S(1)} %get-tuple-element.325), channel_id=1, source_target_pairs={{0,104},{4,108},{8,112},{12,116},{16,120},{20,124},{24,0},{28,4},{... | collective-permute-start | bytes 294920 | tf_op jit(solution)/shard_map/cond/branch_5_fun/ppermute | solution.py:29
  22.2 4.2 %stream.34 = (f32[48,1024]{1,0:T(8,128)S(1)}, s32[2,32,1024]{2,1,0:T(8,128)S(1)}) custom-call(bf16[48,1024]{1,0:T(8,128)(2,1)S(1)} %get-tuple-element.326.z_ref, f32[48,1024]{1,0:T(8,128)S(1)} %get-tuple-element.327.self_ref, s32[4096,1024]{1,0:T(8,128)} %get-tuple-element.328.e2_ref, s32[1,4]{1,0:T(1,128)} %get-tuple-element.329.live_ref), custom_call_target="tpu_custom_call" | custom-call | flops 104857600 | bytes 8388608 | tf_op jit(solution)/shard_map/cond/branch_5_fun/stream/pallas_call | solution.py:335
  26.4 0.2 collective-permute-done.5
  26.6 0.0 collective-permute-done.33.z1_ref
  26.7 0.0 collective-permute-done.32.z2_ref
  26.7 0.0 copy-done
  26.7 1.6 %second.1 = (f32[1,1024]{1,0:T(1,128)S(1)}, f32[32,1,128]{2,1,0:T(1,128)S(1)}) custom-call(bf16[48,1024]{1,0:T(8,128)(2,1)S(1)} %collective-permute-done.32.z2_ref, bf16[48,1024]{1,0:T(8,128)(2,1)S(1)} %collective-permute-done.33.z1_ref, bf16[48,1024]{1,0:T(8,128)(2,1)} %get-tuple-element.515.z3_hbm, f32[48,1024]{1,0:T(8,128)S(1)} %get-tuple-element.516.total_ref, ...), custom_call_target="tpu_custom_call" | custom-call | flops 402653184 | bytes 2097152 | tf_op jit(solution)/shard_map/second/pallas_call | solution.py:367
  28.3 12.4 %all_to_all.5.parts_ref = f32[32,1,128]{2,1,0:T(1,128)S(1)} all-to-all(f32[32,1,128]{2,1,0:T(1,128)S(1)} %get-tuple-element.520), channel_id=1, replica_groups=mesh['node'=32,'feat'=4] {'node'}, dimensions={0} | all-to-all | bytes 32768 | tf_op jit(solution)/shard_map/all_to_all | solution.py:389
  40.7 0.7 %final.1 = (f32[1,1024]{1,0:T(1,128)}, f32[1,1]{1,0:T(1,128)}) custom-call(f32[1,1024]{1,0:T(1,128)S(1)} %get-tuple-element.519.loss_ref, f32[32,1,128]{2,1,0:T(1,128)S(1)} %all_to_all.5.parts_ref), custom_call_target="tpu_custom_call" | custom-call | tf_op jit(solution)/shard_map/final/pallas_call | solution.py:390
Async XLA Ops:
  1.6 10.6 %collective-permute-start.31 = (bf16[32,1792]{1,0:T(8,128)(2,1)S(1)}, bf16[32,1792]{1,0:T(8,128)(2,1)S(1)}, u32[]{:S(2)}, u32[]{:S(2)}) collective-permute-start(bf16[32,1792]{1,0:T(8,128)(2,1)S(1)} %pack.1.after_ref.p0_ref), channel_id=1, source_target_pairs={{0,3},{1,0},{2,1},{3,2},{4,7},{5,4},{6,5},{7,6},{8,11},{9,8},{10,9... | collective-permute-start | bytes 344072 | tf_op jit(solution)/shard_map/ppermute | solution.py:29
  5.3 8.0 %collective-permute-start.30 = (bf16[32,1792]{1,0:T(8,128)(2,1)S(1)}, bf16[32,1792]{1,0:T(8,128)(2,1)S(1)}, u32[]{:S(2)}, u32[]{:S(2)}) collective-permute-start(bf16[32,1792]{1,0:T(8,128)(2,1)S(1)} %pack.1.after_ref.p0_ref), channel_id=1, source_target_pairs={{0,1},{1,2},{2,3},{3,0},{4,5},{5,6},{6,7},{7,4},{8,9},{9,10},{10,1... | collective-permute-start | bytes 344072 | tf_op jit(solution)/shard_map/ppermute | solution.py:29
  5.3 8.0 %collective-permute-start.29 = (bf16[32,1792]{1,0:T(8,128)(2,1)S(1)}, bf16[32,1792]{1,0:T(8,128)(2,1)S(1)}, u32[]{:S(2)}, u32[]{:S(2)}) collective-permute-start(bf16[32,1792]{1,0:T(8,128)(2,1)S(1)} %pack.1.after_ref.p0_ref), channel_id=1, source_target_pairs={{0,2},{1,3},{2,0},{3,1},{4,6},{5,7},{6,4},{7,5},{8,10},{9,11},{10,... | collective-permute-start | bytes 344072 | tf_op jit(solution)/shard_map/ppermute | solution.py:29
  14.1 12.5 %collective-permute-start.33 = (bf16[48,1024]{1,0:T(8,128)(2,1)S(1)}, bf16[48,1024]{1,0:T(8,128)(2,1)S(1)}, u32[]{:S(2)}, u32[]{:S(2)}) collective-permute-start(bf16[48,1024]{1,0:T(8,128)(2,1)S(1)} %get-tuple-element.511), channel_id=1, source_target_pairs={{0,64},{4,68},{8,72},{12,76},{16,80},{20,84},{24,88},{28,92},{32,9... | collective-permute-start | bytes 294920 | tf_op jit(solution)/shard_map/ppermute | solution.py:29
  17.0 9.7 %collective-permute-start.32 = (bf16[48,1024]{1,0:T(8,128)(2,1)S(1)}, bf16[48,1024]{1,0:T(8,128)(2,1)S(1)}, u32[]{:S(2)}, u32[]{:S(2)}) collective-permute-start(bf16[48,1024]{1,0:T(8,128)(2,1)S(1)} %get-tuple-element.511), channel_id=1, source_target_pairs={{0,4},{4,8},{8,12},{12,16},{16,20},{20,24},{24,28},{28,32},{32,36}... | collective-permute-start | bytes 294920 | tf_op jit(solution)/shard_map/ppermute | solution.py:29
  20.0 6.7 %copy-start = (s32[1024]{0:T(1024)S(1)}, s32[1024]{0:T(1024)}, u32[]{:S(2)}) copy-start(s32[1024]{0:T(1024)} %param.48) | copy-start | bytes 12292
  20.0 6.7 %collective-permute-start.5 = (bf16[48,1024]{1,0:T(8,128)(2,1)S(1)}, bf16[48,1024]{1,0:T(8,128)(2,1)}, u32[]{:S(2)}, u32[]{:S(2)}) collective-permute-start(bf16[48,1024]{1,0:T(8,128)(2,1)S(1)} %get-tuple-element.325), channel_id=1, source_target_pairs={{0,104},{4,108},{8,112},{12,116},{16,120},{20,124},{24,0},{28,4},{... | collective-permute-start | bytes 294920 | tf_op jit(solution)/shard_map/cond/branch_5_fun/ppermute | solution.py:29

commit v4 on v3

--- a/solution.py
+++ b/solution.py
@@ -11,12 +11,23 @@
 FAN2 = 10
 LANES = 128
 WORDS = 32
-EARLY = 2
+EARLY = 1
 MIB = 1 << 20
 
 VMEM = pl.BlockSpec(memory_space=pltpu.VMEM)
 HBM = pl.BlockSpec(memory_space=pltpu.HBM)
 SMEM = pl.BlockSpec(memory_space=pltpu.SMEM)
+
+
+def switch_in_range(number, branches, *operands):
+    traced = jax.make_jaxpr(lambda index, *rest: lax.switch(index, branches, *rest))(
+        number, *operands
+    )
+    known = dict(zip(traced.jaxpr.invars, (number, *operands)))
+    known.update(zip(traced.jaxpr.constvars, traced.consts))
+    (chosen,) = [each for each in traced.jaxpr.eqns if each.primitive.name == "cond"]
+    values = [known[each] for each in chosen.invars[1:]]
+    return chosen.primitive.bind(number, *values, **chosen.params)
 
 
 def in_hbm(value):
@@ -155,7 +166,7 @@
 
 
 def first_kernel(
-    hid, depth, p0_ref, p2_ref, p3_ref, p1_ref, e_ref, after_ref, self_ref, z_ref, send_ref, own_ref, x, w1, w2
+    hid, depth, p0_ref, p2_ref, p3_ref, p1_ref, e_ref, self_ref, z_ref, send_ref, own_ref, x, w1, w2
 ):
     me = lax.axis_index("feat")
     height = p0_ref.shape[0]
@@ -303,7 +314,6 @@
     )(*map(in_hbm, (edges_one, edges_two, need_blocks, live_slots)), packed)
     taken = (0, nodes // 2, nodes - 1)
     steps = [step for step in range(nodes) if step not in taken]
-    number = lax.clamp(0, number[0], len(steps) - 1)
 
     self_term, mine, send, own = pl.pallas_call(
         functools.partial(first_kernel, hid, depth),
@@ -313,7 +323,7 @@
             jax.ShapeDtypeStruct((padded, block_len), jnp.bfloat16),
             jax.ShapeDtypeStruct((padded, block_len), jnp.bfloat16),
         ),
-        in_specs=[VMEM] * 5 + [HBM],
+        in_specs=[VMEM] * 5,
         out_specs=(VMEM,) * 4,
         scratch_shapes=[
             pltpu.VMEM((feats * height, block_len), jnp.bfloat16),
@@ -325,7 +335,7 @@
             flops=2 * 128 * block_len * block_len, bytes_accessed=4 * MIB, transcendentals=0
         ),
         name="first",
-    )(*blocks, adjacency, in_hbm(number[None]))
+    )(*blocks, adjacency)
 
     behind = from_ahead(mine, "node", nodes - 1)
     half = from_ahead(mine, "node", nodes // 2)
@@ -354,8 +364,8 @@
         )(own, self_term, in_hbm(edges_two), in_hbm(live_slots))
         return fourth, total, bits_two
 
-    fourth, total, bits_two = lax.switch(
-        number,
+    fourth, total, bits_two = switch_in_range(
+        number[0],
         [functools.partial(with_offset, step) for step in steps],
         send,
         own,

time: 42.3 us -> 42.8 us (1.012)
  loops' own time: 0.01 us -> 0.89 us
  waiting for transfers between devices: 1.32 us -> 1.99 us
  between operations: 1.49 us -> 0.87 us
    another operation x1, loops' own time: 0.01 us -> 0.89 us  [switch_in_range(): return chosen.primitive.bind(number, *values, **chosen.params)]
    ppermute x6, waiting for transfers between devices: 1.32 us -> 1.99 us  [from_ahead(): return lax.ppermute(value, axis, pairs)]
  transfers between devices with their start and end apart: 6 -> 6, of which waited for: 2 -> 1; matrix products, arithmetic and copies ran while one was open for 0% -> 0% of each run, Pallas kernels for 21% -> 21%
where the time goes in v4:
time: 42.8 us; the launch traced here: 42.3 us
  starting transfers between devices  13.4 us (31%)
  Pallas kernels  13.1 us (31%)
  blocking collectives  12.1 us (28%)
  waiting for transfers between devices  1.99 us (5%)
  loops' own time  0.89 us (2%)
  between operations  0.87 us (2%)
    ppermute x6, starting transfers between devices, from_ahead(): return lax.ppermute(value, axis, pairs)  13.4 us
    all_to_all x1, blocking collectives, local(): everyone = lax.all_to_all(sums, 'node', 0, 0, tiled=True)  12.1 us
    pallas_call x1, Pallas kernels, with_offset(): pl.pallas_call(stream_kernel, out_shape=(jax.ShapeDtypeStruct((padded, bl...  4.53 us
    pallas_call x1, Pallas kernels, local(): pl.pallas_call(functools.partial(load_kernel, nodes), out_shape=(jax.Shap...  4.41 us
    ppermute x6, waiting for transfers between devices, from_ahead(): return lax.ppermute(value, axis, pairs)  1.99 us
    pallas_call x1, Pallas kernels, local(): pl.pallas_call(functools.partial(second_kernel, classes), out_shape=(jax....  1.64 us
    pallas_call x1, Pallas kernels, local(): pl.pallas_call(pack_kernel, out_shape=jax.ShapeDtypeStruct((height, width...  0.99 us
    another operation x1, loops' own time, switch_in_range(): return chosen.primitive.bind(number, *values, **chosen.params)  0.89 us
  transfers between devices with their start and end apart: 6, of which 1 were waited for; matrix products, arithmetic and copies ran while one was open for 0% of the time, Pallas kernels for 21%

profile of v4, /device:TPU:1, one launch (start us, length us, event | category | flops | bytes accessed | tf_op | source)
XLA Modules:
  0.0 42.3 jit_solution(7306946962601547078)
XLA Ops:
  0.6 1.0 %pack.1.after_ref.p0_ref = bf16[32,1792]{1,0:T(8,128)(2,1)S(1)} custom-call(bf16[25,1024]{1,0:T(8,128)(2,1)} %refs_0_.1, bf16[25,256]{1,0:T(8,128)(2,1)} %refs_1_.1, bf16[25,256]{1,0:T(8,128)(2,1)} %refs_2_.1, bf16[47,64]{1,0:T(8,128)(2,1)} %bitcast.7, bf16[47,64]{1,0:T(8,128)(2,1)} %bitcast.8), custom_call_target="tpu_custom_call" | custom-call | flops 2097152 | bytes 262144 | tf_op jit(solution)/shard_map/pack/pallas_call | solution.py:274
  1.6 3.6 %collective-permute-start.31 = (bf16[32,1792]{1,0:T(8,128)(2,1)S(1)}, bf16[32,1792]{1,0:T(8,128)(2,1)S(1)}, u32[]{:S(2)}, u32[]{:S(2)}) collective-permute-start(bf16[32,1792]{1,0:T(8,128)(2,1)S(1)} %pack.1.after_ref.p0_ref), channel_id=1, source_target_pairs={{0,3},{1,0},{2,1},{3,2},{4,7},{5,4},{6,5},{7,6},{8,11},{9,8},{10,9... | collective-permute-start | bytes 344072 | tf_op jit(solution)/shard_map/ppermute | solution.py:40
  5.3 0.0 collective-permute-start.30
  5.3 1.6 %collective-permute-start.29 = (bf16[32,1792]{1,0:T(8,128)(2,1)S(1)}, bf16[32,1792]{1,0:T(8,128)(2,1)S(1)}, u32[]{:S(2)}, u32[]{:S(2)}) collective-permute-start(bf16[32,1792]{1,0:T(8,128)(2,1)S(1)} %pack.1.after_ref.p0_ref), channel_id=1, source_target_pairs={{0,2},{1,3},{2,0},{3,1},{4,6},{5,7},{6,4},{7,5},{8,10},{9,11},{10,... | collective-permute-start | bytes 344072 | tf_op jit(solution)/shard_map/ppermute | solution.py:40
  6.9 4.4 %load.1 = (bf16[1024,1024]{1,0:T(8,128)(2,1)S(1)}, s32[2,32,1024]{2,1,0:T(8,128)S(1)}, s32[1]{0:T(128)}) custom-call(s32[1024,1024]{1,0:T(8,128)} %e1_ref.1, s32[4096,1024]{1,0:T(8,128)} %e2_ref.1, s32[1,4]{1,0:T(1,128)} %need_ref.1, s32[1,4]{1,0:T(1,128)} %live_ref.1, bf16[32,1792]{1,0:T(8,128)(2,1)S(1)} %pack.1.after_ref.p0_ref), custom_call_target="tpu_custom_call" | custom-call | flops 104857600 | bytes 10485760 | tf_op jit(solution)/shard_map/load/pallas_call | solution.py:296
  11.3 0.0 collective-permute-done.31.p1_ref
  11.3 1.9 %collective-permute-done.30.p3_ref = bf16[32,1792]{1,0:T(8,128)(2,1)S(1)} collective-permute-done((bf16[32,1792]{1,0:T(8,128)(2,1)S(1)}, bf16[32,1792]{1,0:T(8,128)(2,1)S(1)}, u32[]{:S(2)}, u32[]{:S(2)}) %collective-permute-start.30) | collective-permute-done | bytes 114720 | tf_op jit(solution)/shard_map/ppermute | solution.py:40
  13.3 0.0 collective-permute-done.29.p2_ref
  13.3 0.9 %first.1 = (f32[48,1024]{1,0:T(8,128)S(1)}, bf16[48,1024]{1,0:T(8,128)(2,1)S(1)}, bf16[48,1024]{1,0:T(8,128)(2,1)S(1)}, bf16[48,1024]{1,0:T(8,128)(2,1)S(1)}) custom-call(bf16[32,1792]{1,0:T(8,128)(2,1)S(1)} %pack.1.after_ref.p0_ref, bf16[32,1792]{1,0:T(8,128)(2,1)S(1)} %collective-permute-done.29.p2_ref, ...), custom_call_target="tpu_custom_call" | custom-call | flops 268435456 | bytes 4194304 | tf_op jit(solution)/shard_map/first/pallas_call | solution.py:318
  14.1 2.8 %collective-permute-start.33 = (bf16[48,1024]{1,0:T(8,128)(2,1)S(1)}, bf16[48,1024]{1,0:T(8,128)(2,1)S(1)}, u32[]{:S(2)}, u32[]{:S(2)}) collective-permute-start(bf16[48,1024]{1,0:T(8,128)(2,1)S(1)} %get-tuple-element.510), channel_id=1, source_target_pairs={{0,64},{4,68},{8,72},{12,76},{16,80},{20,84},{24,88},{28,92},{32,9... | collective-permute-start | bytes 294920 | tf_op jit(solution)/shard_map/ppermute | solution.py:40
  17.0 3.0 %collective-permute-start.32 = (bf16[48,1024]{1,0:T(8,128)(2,1)S(1)}, bf16[48,1024]{1,0:T(8,128)(2,1)S(1)}, u32[]{:S(2)}, u32[]{:S(2)}) collective-permute-start(bf16[48,1024]{1,0:T(8,128)(2,1)S(1)} %get-tuple-element.510), channel_id=1, source_target_pairs={{0,4},{4,8},{8,12},{12,16},{16,20},{20,24},{24,28},{28,32},{32,36}... | collective-permute-start | bytes 294920 | tf_op jit(solution)/shard_map/ppermute | solution.py:40
  20.0 0.0 copy-start
  20.0 7.7 %conditional.1 = (bf16[48,1024]{1,0:T(8,128)(2,1)}, f32[48,1024]{1,0:T(8,128)S(1)}, s32[2,32,1024]{2,1,0:T(8,128)S(1)}) conditional(s32[]{:T(128)} %bitcast.2, (bf16[48,1024]{1,0:T(8,128)(2,1)S(1)}, bf16[48,1024]{1,0:T(8,128)(2,1)S(1)}, f32[48,1024]{1,0:T(8,128)S(1)}, s32[4096,1024]{1,0:T(8,128)}, ...), branch_computations={%region_0.0_spmd, %region_1.0_spmd, %region_2.0_spmd, %region_3.0_... | conditional | flops 104857600 | bytes 8781888 | solution.py:30
  20.7 2.3 %collective-permute-start.5 = (bf16[48,1024]{1,0:T(8,128)(2,1)S(1)}, bf16[48,1024]{1,0:T(8,128)(2,1)}, u32[]{:S(2)}, u32[]{:S(2)}) collective-permute-start(bf16[48,1024]{1,0:T(8,128)(2,1)S(1)} %get-tuple-element.325), channel_id=1, source_target_pairs={{0,104},{4,108},{8,112},{12,116},{16,120},{20,124},{24,0},{28,4},{... | collective-permute-start | bytes 294920 | tf_op jit(solution)/shard_map/cond/branch_5_fun/ppermute | solution.py:40
  23.0 4.5 %stream.34 = (f32[48,1024]{1,0:T(8,128)S(1)}, s32[2,32,1024]{2,1,0:T(8,128)S(1)}) custom-call(bf16[48,1024]{1,0:T(8,128)(2,1)S(1)} %get-tuple-element.326.z_ref, f32[48,1024]{1,0:T(8,128)S(1)} %get-tuple-element.327.self_ref, s32[4096,1024]{1,0:T(8,128)} %get-tuple-element.328.e2_ref, s32[1,4]{1,0:T(1,128)} %get-tuple-element.329.live_ref), custom_call_target="tpu_custom_call" | custom-call | flops 104857600 | bytes 8388608 | tf_op jit(solution)/shard_map/cond/branch_5_fun/stream/pallas_call | solution.py:345
  27.5 0.0 collective-permute-done.5
  27.7 0.0 collective-permute-done.33.z1_ref
  27.7 0.0 collective-permute-done.32.z2_ref
  27.7 0.0 copy-done
  27.7 1.6 %second.1 = (f32[1,1024]{1,0:T(1,128)S(1)}, f32[32,1,128]{2,1,0:T(1,128)S(1)}) custom-call(bf16[48,1024]{1,0:T(8,128)(2,1)S(1)} %collective-permute-done.32.z2_ref, bf16[48,1024]{1,0:T(8,128)(2,1)S(1)} %collective-permute-done.33.z1_ref, bf16[48,1024]{1,0:T(8,128)(2,1)} %get-tuple-element.515.z3_hbm, f32[48,1024]{1,0:T(8,128)S(1)} %get-tuple-element.516.total_ref, ...), custom_call_target="tpu_custom_call" | custom-call | flops 402653184 | bytes 2097152 | tf_op jit(solution)/shard_map/second/pallas_call | solution.py:377
  29.4 12.1 %all_to_all.5.parts_ref = f32[32,1,128]{2,1,0:T(1,128)S(1)} all-to-all(f32[32,1,128]{2,1,0:T(1,128)S(1)} %get-tuple-element.520), channel_id=1, replica_groups=mesh['node'=32,'feat'=4] {'node'}, dimensions={0} | all-to-all | bytes 32768 | tf_op jit(solution)/shard_map/all_to_all | solution.py:399
  41.5 0.7 %final.1 = (f32[1,1024]{1,0:T(1,128)}, f32[1,1]{1,0:T(1,128)}) custom-call(f32[1,1024]{1,0:T(1,128)S(1)} %get-tuple-element.519.loss_ref, f32[32,1,128]{2,1,0:T(1,128)S(1)} %all_to_all.5.parts_ref), custom_call_target="tpu_custom_call" | custom-call | tf_op jit(solution)/shard_map/final/pallas_call | solution.py:400
Async XLA Ops:
  1.6 9.7 %collective-permute-start.31 = (bf16[32,1792]{1,0:T(8,128)(2,1)S(1)}, bf16[32,1792]{1,0:T(8,128)(2,1)S(1)}, u32[]{:S(2)}, u32[]{:S(2)}) collective-permute-start(bf16[32,1792]{1,0:T(8,128)(2,1)S(1)} %pack.1.after_ref.p0_ref), channel_id=1, source_target_pairs={{0,3},{1,0},{2,1},{3,2},{4,7},{5,4},{6,5},{7,6},{8,11},{9,8},{10,9... | collective-permute-start | bytes 344072 | tf_op jit(solution)/shard_map/ppermute | solution.py:40
  5.3 8.0 %collective-permute-start.30 = (bf16[32,1792]{1,0:T(8,128)(2,1)S(1)}, bf16[32,1792]{1,0:T(8,128)(2,1)S(1)}, u32[]{:S(2)}, u32[]{:S(2)}) collective-permute-start(bf16[32,1792]{1,0:T(8,128)(2,1)S(1)} %pack.1.after_ref.p0_ref), channel_id=1, source_target_pairs={{0,1},{1,2},{2,3},{3,0},{4,5},{5,6},{6,7},{7,4},{8,9},{9,10},{10,1... | collective-permute-start | bytes 344072 | tf_op jit(solution)/shard_map/ppermute | solution.py:40
  5.3 8.0 %collective-permute-start.29 = (bf16[32,1792]{1,0:T(8,128)(2,1)S(1)}, bf16[32,1792]{1,0:T(8,128)(2,1)S(1)}, u32[]{:S(2)}, u32[]{:S(2)}) collective-permute-start(bf16[32,1792]{1,0:T(8,128)(2,1)S(1)} %pack.1.after_ref.p0_ref), channel_id=1, source_target_pairs={{0,2},{1,3},{2,0},{3,1},{4,6},{5,7},{6,4},{7,5},{8,10},{9,11},{10,... | collective-permute-start | bytes 344072 | tf_op jit(solution)/shard_map/ppermute | solution.py:40
  14.1 13.6 %collective-permute-start.33 = (bf16[48,1024]{1,0:T(8,128)(2,1)S(1)}, bf16[48,1024]{1,0:T(8,128)(2,1)S(1)}, u32[]{:S(2)}, u32[]{:S(2)}) collective-permute-start(bf16[48,1024]{1,0:T(8,128)(2,1)S(1)} %get-tuple-element.510), channel_id=1, source_target_pairs={{0,64},{4,68},{8,72},{12,76},{16,80},{20,84},{24,88},{28,92},{32,9... | collective-permute-start | bytes 294920 | tf_op jit(solution)/shard_map/ppermute | solution.py:40
  17.0 10.8 %collective-permute-start.32 = (bf16[48,1024]{1,0:T(8,128)(2,1)S(1)}, bf16[48,1024]{1,0:T(8,128)(2,1)S(1)}, u32[]{:S(2)}, u32[]{:S(2)}) collective-permute-start(bf16[48,1024]{1,0:T(8,128)(2,1)S(1)} %get-tuple-element.510), channel_id=1, source_target_pairs={{0,4},{4,8},{8,12},{12,16},{16,20},{20,24},{24,28},{28,32},{32,36}... | collective-permute-start | bytes 294920 | tf_op jit(solution)/shard_map/ppermute | solution.py:40
  20.0 7.8 %copy-start = (s32[1024]{0:T(1024)S(1)}, s32[1024]{0:T(1024)}, u32[]{:S(2)}) copy-start(s32[1024]{0:T(1024)} %param.48) | copy-start | bytes 12292
  20.7 6.8 %collective-permute-start.5 = (bf16[48,1024]{1,0:T(8,128)(2,1)S(1)}, bf16[48,1024]{1,0:T(8,128)(2,1)}, u32[]{:S(2)}, u32[]{:S(2)}) collective-permute-start(bf16[48,1024]{1,0:T(8,128)(2,1)S(1)} %get-tuple-element.325), channel_id=1, source_target_pairs={{0,104},{4,108},{8,112},{12,116},{16,120},{20,124},{24,0},{28,4},{... | collective-permute-start | bytes 294920 | tf_op jit(solution)/shard_map/cond/branch_5_fun/ppermute | solution.py:40

commit v5 on v3

--- a/solution.py
+++ b/solution.py
@@ -77,7 +77,7 @@
 
 
 def load_kernel(
-    nodes, e1_ref, e2_ref, need_ref, live_ref, after_ref, e1_out, bits_ref, number_ref, need, live, held, sems
+    nodes, e1_ref, e2_ref, need_ref, live_ref, after_ref, e1_out, bits_ref, number_ref, need, live, number, held, sems
 ):
     rows = held.shape[1]
     cols = e1_out.shape[0]
@@ -99,7 +99,9 @@
     for copy in small:
         copy.wait()
     offset = lax.rem(need[0, 3] - lax.axis_index("node") + nodes, nodes)
-    number_ref[0] = offset - 1 - (offset > nodes // 2).astype(jnp.int32)
+    number[0] = offset - 1 - (offset > nodes // 2).astype(jnp.int32)
+    told = pltpu.make_async_copy(number, number_ref, sems.at[len(sources) + 2])
+    told.start()
 
     def arrived(index):
         copies[index].wait()
@@ -111,6 +113,7 @@
     for place, slot, begin, count in ((0, 1, per_slot, per_slot), (1, 3, 2 * per_slot, extra)):
         pieces = [functools.partial(arrived, begin + index) for index in range(count)]
         bits_ref[place] = jnp.where(live[0, slot] == 1, pack_slot(pieces, 0), 0)
+    told.wait()
 
 
 def stream_kernel(z_ref, self_ref, e2_ref, live_ref, total_ref, bits_ref, held, acc, live, sems):
@@ -155,7 +158,7 @@
 
 
 def first_kernel(
-    hid, depth, p0_ref, p2_ref, p3_ref, p1_ref, e_ref, after_ref, self_ref, z_ref, send_ref, own_ref, x, w1, w2
+    hid, depth, p0_ref, p2_ref, p1_ref, p3_ref, e_ref, after_ref, self_ref, z_ref, send_ref, own_ref, x, w1, w2
 ):
     me = lax.axis_index("feat")
     height = p0_ref.shape[0]
@@ -195,11 +198,9 @@
 
 
 def second_kernel(
-    classes, z2_ref, z1_ref, z3_hbm, total_ref, b13_ref, b23_ref, label_ref, loss_ref, sum_ref, z3_ref, acc, sem
+    classes, z2_ref, z1_ref, z3_ref, total_ref, b13_ref, b23_ref, label_ref, loss_ref, sum_ref, acc
 ):
     padded, cols = total_ref.shape
-    fetch = pltpu.make_async_copy(z3_hbm, z3_ref, sem)
-    fetch.start()
     chunk = 256
 
     def edges(words):
@@ -215,7 +216,6 @@
         acc[:, part] = term + jnp.dot(
             z2_ref[...], edges(b23_ref[0, :, part]), preferred_element_type=jnp.float32
         )
-    fetch.wait()
     class_ids = lax.broadcasted_iota(jnp.int32, (padded, chunk), 0)
     summed = jnp.zeros((1, chunk), jnp.float32)
     for first in range(0, cols, chunk):
@@ -232,6 +232,10 @@
         summed = summed + loss
     mean = jnp.sum(summed, keepdims=True) / (cols * sum_ref.shape[0])
     sum_ref[...] = jnp.broadcast_to(mean.reshape(1, 1, 1), sum_ref.shape)
+
+
+def hand_on_kernel(in_ref, out_ref):
+    out_ref[...] = in_ref[...]
 
 
 def final_kernel(loss_ref, parts_ref, out_ref, mean_ref):
@@ -280,7 +284,7 @@
         name="pack",
     )(*map(in_hbm, (features, w1_self, w1_nbr, w2_self.T, w2_nbr.T)))
 
-    blocks = [packed] + [from_ahead(packed, "feat", step) for step in (2, 3, 1)]
+    blocks = [packed] + [from_ahead(packed, "feat", step) for step in (2, 1, 3)]
     words = block_len // 32
     adjacency, bits_outer, number = pl.pallas_call(
         functools.partial(load_kernel, nodes),
@@ -290,12 +294,13 @@
             jax.ShapeDtypeStruct((1,), jnp.int32),
         ),
         in_specs=[HBM] * 4 + [VMEM],
-        out_specs=(VMEM, VMEM, SMEM),
+        out_specs=(VMEM, VMEM, HBM),
         scratch_shapes=[
             pltpu.SMEM(need_blocks.shape, jnp.int32),
             pltpu.SMEM(live_slots.shape, jnp.int32),
+            pltpu.SMEM((1,), jnp.int32),
             pltpu.VMEM((8 + EARLY, block_len // 4, block_len), jnp.int32),
-            pltpu.SemaphoreType.DMA((10 + EARLY,)),
+            pltpu.SemaphoreType.DMA((11 + EARLY,)),
         ],
         compiler_params=pltpu.CompilerParams(vmem_limit_bytes=16 * MIB),
         cost_estimate=pl.CostEstimate(flops=100 * MIB, bytes_accessed=10 * MIB, transcendentals=0),
@@ -352,6 +357,14 @@
             ),
             name="stream",
         )(own, self_term, in_hbm(edges_two), in_hbm(live_slots))
+        fourth = pl.pallas_call(
+            hand_on_kernel,
+            out_shape=jax.ShapeDtypeStruct(fourth.shape, fourth.dtype),
+            in_specs=[VMEM],
+            out_specs=VMEM,
+            compiler_params=pltpu.CompilerParams(vmem_limit_bytes=1 * MIB),
+            name="hand_on",
+        )(fourth)
         return fourth, total, bits_two
 
     fourth, total, bits_two = lax.switch(
@@ -370,13 +383,9 @@
             jax.ShapeDtypeStruct((1, block_len), jnp.float32),
             jax.ShapeDtypeStruct((nodes, 1, LANES), jnp.float32),
         ),
-        in_specs=[VMEM, VMEM, HBM] + [VMEM] * 4,
+        in_specs=[VMEM] * 7,
         out_specs=(VMEM, VMEM),
-        scratch_shapes=[
-            pltpu.VMEM((padded, block_len), jnp.bfloat16),
-            pltpu.VMEM((padded, block_len), jnp.float32),
-            pltpu.SemaphoreType.DMA,
-        ],
+        scratch_shapes=[pltpu.VMEM((padded, block_len), jnp.float32)],
         compiler_params=pltpu.CompilerParams(vmem_limit_bytes=16 * MIB),
         cost_estimate=pl.CostEstimate(
             flops=2 * 64 * 3 * block_len * block_len,
@@ -384,7 +393,7 @@
             transcendentals=padded * block_len,
         ),
         name="second",
-    )(behind, half, in_hbm(fourth), total, bits_outer, bits_two, labels[None, :])
+    )(behind, half, fourth, total, bits_outer, bits_two, labels[None, :])
 
     everyone = lax.all_to_all(sums, "node", 0, 0, tiled=True)
     node_loss, mean_loss = pl.pallas_call(

time: 42.3 us -> 40.9 us (0.967); the launches traced: 41.5 us -> 41.6 us
  waiting for transfers between devices: 1.32 us -> 0.02 us
  blocking collectives: 12.4 us -> 13.2 us
  starting transfers between devices: 13.3 us -> 14.1 us
  Pallas kernels: 13 us -> 12.5 us
    ppermute x6, waiting for transfers between devices: 1.32 us -> 0.02 us  [from_ahead(): return lax.ppermute(value, axis, pairs)]
    all_to_all x1, blocking collectives: 12.4 us -> 13.2 us  [local(): everyone = lax.all_to_all(sums, 'node', 0, 0, tiled=True)]
    ppermute x6, starting transfers between devices: 13.3 us -> 14.1 us  [from_ahead(): return lax.ppermute(value, axis, pairs)]
    pallas_call x1, Pallas kernels: 4.63 us -> 4.2 us  [local(): pl.pallas_call(functools.partial(load_kernel, nodes), out_shape=(jax.Shap...]
  transfers between devices with their start and end apart: 6 -> 6, of which waited for: 2 -> 0; matrix products, arithmetic and copies ran while one was open for 0% -> 0% of each run, Pallas kernels for 21% -> 20%
where the time goes in v5:
time: 40.9 us; the launch traced here: 41.6 us
  starting transfers between devices  14.1 us (34%)
  blocking collectives  13.2 us (32%)
  Pallas kernels  12.5 us (31%)
  between operations  1.53 us (4%)
    ppermute x6, starting transfers between devices, from_ahead(): return lax.ppermute(value, axis, pairs)  14.1 us
    all_to_all x1, blocking collectives, local(): everyone = lax.all_to_all(sums, 'node', 0, 0, tiled=True)  13.2 us
    pallas_call x1, Pallas kernels, with_offset(): pl.pallas_call(stream_kernel, out_shape=(jax.ShapeDtypeStruct((padded, bl...  4.22 us
    pallas_call x1, Pallas kernels, local(): pl.pallas_call(functools.partial(load_kernel, nodes), out_shape=(jax.Shap...  4.2 us
    pallas_call x1, Pallas kernels, local(): pl.pallas_call(functools.partial(second_kernel, classes), out_shape=(jax....  1.59 us
    pallas_call x1, Pallas kernels, local(): pl.pallas_call(pack_kernel, out_shape=jax.ShapeDtypeStruct((height, width...  0.99 us
    pallas_call x1, Pallas kernels, local(): pl.pallas_call(functools.partial(first_kernel, hid, depth), out_shape=(ja...  0.85 us
  transfers between devices with their start and end apart: 6, of which 0 were waited for; matrix products, arithmetic and copies ran while one was open for 0% of the time, Pallas kernels for 20%

profile of v5, /device:TPU:1, one launch (start us, length us, event | category | flops | bytes accessed | tf_op | source)
XLA Modules:
  0.0 41.6 jit_solution(4867081379943863184)
XLA Ops:
  0.6 1.0 %pack.1.after_ref.p0_ref = bf16[32,1792]{1,0:T(8,128)(2,1)S(1)} custom-call(bf16[25,1024]{1,0:T(8,128)(2,1)} %refs_0_.1, bf16[25,256]{1,0:T(8,128)(2,1)} %refs_1_.1, bf16[25,256]{1,0:T(8,128)(2,1)} %refs_2_.1, bf16[47,64]{1,0:T(8,128)(2,1)} %bitcast.7, bf16[47,64]{1,0:T(8,128)(2,1)} %bitcast.8), custom_call_target="tpu_custom_call" | custom-call | flops 2097152 | bytes 262144 | tf_op jit(solution)/shard_map/pack/pallas_call | solution.py:267
  1.6 2.2 %collective-permute-start.31 = (bf16[32,1792]{1,0:T(8,128)(2,1)S(1)}, bf16[32,1792]{1,0:T(8,128)(2,1)S(1)}, u32[]{:S(2)}, u32[]{:S(2)}) collective-permute-start(bf16[32,1792]{1,0:T(8,128)(2,1)S(1)} %pack.1.after_ref.p0_ref), channel_id=1, source_target_pairs={{0,1},{1,2},{2,3},{3,0},{4,5},{5,6},{6,7},{7,4},{8,9},{9,10},{10,1... | collective-permute-start | bytes 344072 | tf_op jit(solution)/shard_map/ppermute | solution.py:29
  3.8 1.5 %collective-permute-start.30 = (bf16[32,1792]{1,0:T(8,128)(2,1)S(1)}, bf16[32,1792]{1,0:T(8,128)(2,1)S(1)}, u32[]{:S(2)}, u32[]{:S(2)}) collective-permute-start(bf16[32,1792]{1,0:T(8,128)(2,1)S(1)} %pack.1.after_ref.p0_ref), channel_id=1, source_target_pairs={{0,3},{1,0},{2,1},{3,2},{4,7},{5,4},{6,5},{7,6},{8,11},{9,8},{10,9... | collective-permute-start | bytes 344072 | tf_op jit(solution)/shard_map/ppermute | solution.py:29
  5.3 1.6 %collective-permute-start.29 = (bf16[32,1792]{1,0:T(8,128)(2,1)S(1)}, bf16[32,1792]{1,0:T(8,128)(2,1)S(1)}, u32[]{:S(2)}, u32[]{:S(2)}) collective-permute-start(bf16[32,1792]{1,0:T(8,128)(2,1)S(1)} %pack.1.after_ref.p0_ref), channel_id=1, source_target_pairs={{0,2},{1,3},{2,0},{3,1},{4,6},{5,7},{6,4},{7,5},{8,10},{9,11},{10,... | collective-permute-start | bytes 344072 | tf_op jit(solution)/shard_map/ppermute | solution.py:29
  6.9 4.2 %load.1 = (bf16[1024,1024]{1,0:T(8,128)(2,1)S(1)}, s32[2,32,1024]{2,1,0:T(8,128)S(1)}, s32[1]{0:T(128)}) custom-call(s32[1024,1024]{1,0:T(8,128)} %e1_ref.1, s32[4096,1024]{1,0:T(8,128)} %e2_ref.1, s32[1,4]{1,0:T(1,128)} %need_ref.1, s32[1,4]{1,0:T(1,128)} %live_ref.1, bf16[32,1792]{1,0:T(8,128)(2,1)S(1)} %pack.1.after_ref.p0_ref), custom_call_target="tpu_custom_call" | custom-call | flops 104857600 | bytes 10485760 | tf_op jit(solution)/shard_map/load/pallas_call | solution.py:289
  11.8 0.0 collective-permute-done.31.p3_ref
  11.8 0.0 collective-permute-done.30.p1_ref
  11.8 0.0 collective-permute-done.29.p2_ref
  11.8 0.9 %first.1 = (f32[48,1024]{1,0:T(8,128)S(1)}, bf16[48,1024]{1,0:T(8,128)(2,1)S(1)}, bf16[48,1024]{1,0:T(8,128)(2,1)S(1)}, bf16[48,1024]{1,0:T(8,128)(2,1)S(1)}) custom-call(bf16[32,1792]{1,0:T(8,128)(2,1)S(1)} %pack.1.after_ref.p0_ref, bf16[32,1792]{1,0:T(8,128)(2,1)S(1)} %collective-permute-done.29.p2_ref, ...), custom_call_target="tpu_custom_call" | custom-call | flops 268435456 | bytes 4194304 | tf_op jit(solution)/shard_map/first/pallas_call | solution.py:313
  12.6 2.8 %collective-permute-start.33 = (bf16[48,1024]{1,0:T(8,128)(2,1)S(1)}, bf16[48,1024]{1,0:T(8,128)(2,1)S(1)}, u32[]{:S(2)}, u32[]{:S(2)}) collective-permute-start(bf16[48,1024]{1,0:T(8,128)(2,1)S(1)} %get-tuple-element.511), channel_id=1, source_target_pairs={{0,64},{4,68},{8,72},{12,76},{16,80},{20,84},{24,88},{28,92},{32,9... | collective-permute-start | bytes 294920 | tf_op jit(solution)/shard_map/ppermute | solution.py:29
  15.5 3.3 %collective-permute-start.32 = (bf16[48,1024]{1,0:T(8,128)(2,1)S(1)}, bf16[48,1024]{1,0:T(8,128)(2,1)S(1)}, u32[]{:S(2)}, u32[]{:S(2)}) collective-permute-start(bf16[48,1024]{1,0:T(8,128)(2,1)S(1)} %get-tuple-element.511), channel_id=1, source_target_pairs={{0,4},{4,8},{8,12},{12,16},{16,20},{20,24},{24,28},{28,32},{32,36}... | collective-permute-start | bytes 294920 | tf_op jit(solution)/shard_map/ppermute | solution.py:29
  18.8 0.0 copy-start
  18.8 7.1 %conditional.1 = (bf16[48,1024]{1,0:T(8,128)(2,1)S(1)}, f32[48,1024]{1,0:T(8,128)S(1)}, s32[2,32,1024]{2,1,0:T(8,128)S(1)}) conditional(s32[]{:T(128)} %bitcast.2, (bf16[48,1024]{1,0:T(8,128)(2,1)S(1)}, bf16[48,1024]{1,0:T(8,128)(2,1)S(1)}, f32[48,1024]{1,0:T(8,128)S(1)}, s32[4096,1024]{1,0:T(8,128)}, ...), branch_computations={%region_0.0_spmd, %region_1.0_spmd, %region_2.0_spmd, %region_3.0_... | conditional | flops 104857600 | bytes 8781888 | solution.py:370
  18.8 2.7 %collective-permute-start.2 = (bf16[48,1024]{1,0:T(8,128)(2,1)S(1)}, bf16[48,1024]{1,0:T(8,128)(2,1)S(1)}, u32[]{:S(2)}, u32[]{:S(2)}) collective-permute-start(bf16[48,1024]{1,0:T(8,128)(2,1)S(1)} %get-tuple-element.304), channel_id=1, source_target_pairs={{0,116},{4,120},{8,124},{12,0},{16,4},{20,8},{24,12},{28,16},{32,2... | collective-permute-start | bytes 294920 | tf_op jit(solution)/shard_map/cond/branch_2_fun/ppermute | solution.py:29
  21.5 4.2 %stream.31 = (f32[48,1024]{1,0:T(8,128)S(1)}, s32[2,32,1024]{2,1,0:T(8,128)S(1)}) custom-call(bf16[48,1024]{1,0:T(8,128)(2,1)S(1)} %get-tuple-element.305.z_ref, f32[48,1024]{1,0:T(8,128)S(1)} %get-tuple-element.306.self_ref, s32[4096,1024]{1,0:T(8,128)} %get-tuple-element.307.e2_ref, s32[1,4]{1,0:T(1,128)} %get-tuple-element.308.live_ref), custom_call_target="tpu_custom_call" | custom-call | flops 104857600 | bytes 8388608 | tf_op jit(solution)/shard_map/cond/branch_2_fun/stream/pallas_call | solution.py:340
  25.7 0.0 collective-permute-done.2.in_ref
  25.9 0.0 collective-permute-done.33.z1_ref
  26.0 0.0 collective-permute-done.32.z2_ref
  26.0 0.0 copy-done
  26.0 1.6 %second.1 = (f32[1,1024]{1,0:T(1,128)S(1)}, f32[32,1,128]{2,1,0:T(1,128)S(1)}) custom-call(bf16[48,1024]{1,0:T(8,128)(2,1)S(1)} %collective-permute-done.32.z2_ref, bf16[48,1024]{1,0:T(8,128)(2,1)S(1)} %collective-permute-done.33.z1_ref, bf16[48,1024]{1,0:T(8,128)(2,1)S(1)} %get-tuple-element.515.z3_ref, f32[48,1024]{1,0:T(8,128)S(1)} %get-tuple-element.516.total_ref, ...), custom_call_target="tpu_custom_call" | custom-call | flops 402653184 | bytes 2097152 | tf_op jit(solution)/shard_map/second/pallas_call | solution.py:380
  27.6 13.2 %all_to_all.5.parts_ref = f32[32,1,128]{2,1,0:T(1,128)S(1)} all-to-all(f32[32,1,128]{2,1,0:T(1,128)S(1)} %get-tuple-element.520), channel_id=1, replica_groups=mesh['node'=32,'feat'=4] {'node'}, dimensions={0} | all-to-all | bytes 32768 | tf_op jit(solution)/shard_map/all_to_all | solution.py:398
  40.8 0.7 %final.1 = (f32[1,1024]{1,0:T(1,128)}, f32[1,1]{1,0:T(1,128)}) custom-call(f32[1,1024]{1,0:T(1,128)S(1)} %get-tuple-element.519.loss_ref, f32[32,1,128]{2,1,0:T(1,128)S(1)} %all_to_all.5.parts_ref), custom_call_target="tpu_custom_call" | custom-call | tf_op jit(solution)/shard_map/final/pallas_call | solution.py:399
  (1 shorter events, 0.0 us)
Async XLA Ops:
  1.6 10.1 %collective-permute-start.31 = (bf16[32,1792]{1,0:T(8,128)(2,1)S(1)}, bf16[32,1792]{1,0:T(8,128)(2,1)S(1)}, u32[]{:S(2)}, u32[]{:S(2)}) collective-permute-start(bf16[32,1792]{1,0:T(8,128)(2,1)S(1)} %pack.1.after_ref.p0_ref), channel_id=1, source_target_pairs={{0,1},{1,2},{2,3},{3,0},{4,5},{5,6},{6,7},{7,4},{8,9},{9,10},{10,1... | collective-permute-start | bytes 344072 | tf_op jit(solution)/shard_map/ppermute | solution.py:29
  3.8 8.0 %collective-permute-start.30 = (bf16[32,1792]{1,0:T(8,128)(2,1)S(1)}, bf16[32,1792]{1,0:T(8,128)(2,1)S(1)}, u32[]{:S(2)}, u32[]{:S(2)}) collective-permute-start(bf16[32,1792]{1,0:T(8,128)(2,1)S(1)} %pack.1.after_ref.p0_ref), channel_id=1, source_target_pairs={{0,3},{1,0},{2,1},{3,2},{4,7},{5,4},{6,5},{7,6},{8,11},{9,8},{10,9... | collective-permute-start | bytes 344072 | tf_op jit(solution)/shard_map/ppermute | solution.py:29
  5.3 6.4 %collective-permute-start.29 = (bf16[32,1792]{1,0:T(8,128)(2,1)S(1)}, bf16[32,1792]{1,0:T(8,128)(2,1)S(1)}, u32[]{:S(2)}, u32[]{:S(2)}) collective-permute-start(bf16[32,1792]{1,0:T(8,128)(2,1)S(1)} %pack.1.after_ref.p0_ref), channel_id=1, source_target_pairs={{0,2},{1,3},{2,0},{3,1},{4,6},{5,7},{6,4},{7,5},{8,10},{9,11},{10,... | collective-permute-start | bytes 344072 | tf_op jit(solution)/shard_map/ppermute | solution.py:29
  12.6 13.3 %collective-permute-start.33 = (bf16[48,1024]{1,0:T(8,128)(2,1)S(1)}, bf16[48,1024]{1,0:T(8,128)(2,1)S(1)}, u32[]{:S(2)}, u32[]{:S(2)}) collective-permute-start(bf16[48,1024]{1,0:T(8,128)(2,1)S(1)} %get-tuple-element.511), channel_id=1, source_target_pairs={{0,64},{4,68},{8,72},{12,76},{16,80},{20,84},{24,88},{28,92},{32,9... | collective-permute-start | bytes 294920 | tf_op jit(solution)/shard_map/ppermute | solution.py:29
  15.5 10.5 %collective-permute-start.32 = (bf16[48,1024]{1,0:T(8,128)(2,1)S(1)}, bf16[48,1024]{1,0:T(8,128)(2,1)S(1)}, u32[]{:S(2)}, u32[]{:S(2)}) collective-permute-start(bf16[48,1024]{1,0:T(8,128)(2,1)S(1)} %get-tuple-element.511), channel_id=1, source_target_pairs={{0,4},{4,8},{8,12},{12,16},{16,20},{20,24},{24,28},{28,32},{32,36}... | collective-permute-start | bytes 294920 | tf_op jit(solution)/shard_map/ppermute | solution.py:29
  18.8 7.2 %copy-start = (s32[1024]{0:T(1024)S(1)}, s32[1024]{0:T(1024)}, u32[]{:S(2)}) copy-start(s32[1024]{0:T(1024)} %param.48) | copy-start | bytes 12292
  18.8 6.9 %collective-permute-start.2 = (bf16[48,1024]{1,0:T(8,128)(2,1)S(1)}, bf16[48,1024]{1,0:T(8,128)(2,1)S(1)}, u32[]{:S(2)}, u32[]{:S(2)}) collective-permute-start(bf16[48,1024]{1,0:T(8,128)(2,1)S(1)} %get-tuple-element.304), channel_id=1, source_target_pairs={{0,116},{4,120},{8,124},{12,0},{16,4},{20,8},{24,12},{28,16},{32,2... | collective-permute-start | bytes 294920 | tf_op jit(solution)/shard_map/cond/branch_2_fun/ppermute | solution.py:29

commit v6 on v5

--- a/solution.py
+++ b/solution.py
@@ -11,7 +11,7 @@
 FAN2 = 10
 LANES = 128
 WORDS = 32
-EARLY = 2
+EARLY = 1
 MIB = 1 << 20
 
 VMEM = pl.BlockSpec(memory_space=pltpu.VMEM)

time: 40.9 us -> 42 us (1.027); the launches traced: 41.6 us -> 41.7 us
  blocking collectives: 13.2 us -> 12 us
  starting transfers between devices: 14.1 us -> 15.1 us
    all_to_all x1, blocking collectives: 13.2 us -> 12 us  [local(): everyone = lax.all_to_all(sums, 'node', 0, 0, tiled=True)]
    ppermute x6, starting transfers between devices: 14.1 us -> 15.1 us  [from_ahead(): return lax.ppermute(value, axis, pairs)]
  transfers between devices with their start and end apart: 6 -> 6, of which waited for: 0 -> 1; matrix products, arithmetic and copies ran while one was open for 0% -> 0% of each run, Pallas kernels for 20% -> 20%
where the time goes in v6:
time: 42 us; the launch traced here: 41.7 us
  starting transfers between devices  15.1 us (36%)
  Pallas kernels  12.6 us (30%)
  blocking collectives  12 us (29%)
  between operations  1.52 us (4%)
    ppermute x6, starting transfers between devices, from_ahead(): return lax.ppermute(value, axis, pairs)  15.1 us
    all_to_all x1, blocking collectives, local(): everyone = lax.all_to_all(sums, 'node', 0, 0, tiled=True)  12 us
    pallas_call x1, Pallas kernels, with_offset(): pl.pallas_call(stream_kernel, out_shape=(jax.ShapeDtypeStruct((padded, bl...  4.53 us
    pallas_call x1, Pallas kernels, local(): pl.pallas_call(functools.partial(load_kernel, nodes), out_shape=(jax.Shap...  3.98 us
    pallas_call x1, Pallas kernels, local(): pl.pallas_call(functools.partial(second_kernel, classes), out_shape=(jax....  1.59 us
    pallas_call x1, Pallas kernels, local(): pl.pallas_call(pack_kernel, out_shape=jax.ShapeDtypeStruct((height, width...  0.99 us
    pallas_call x1, Pallas kernels, local(): pl.pallas_call(functools.partial(first_kernel, hid, depth), out_shape=(ja...  0.85 us
  transfers between devices with their start and end apart: 6, of which 1 were waited for; matrix products, arithmetic and copies ran while one was open for 0% of the time, Pallas kernels for 20%

profile of v6, /device:TPU:1, one launch (start us, length us, event | category | flops | bytes accessed | tf_op | source)
XLA Modules:
  0.0 41.7 jit_solution(2126379274042250928)
XLA Ops:
  0.6 1.0 %pack.1.after_ref.p0_ref = bf16[32,1792]{1,0:T(8,128)(2,1)S(1)} custom-call(bf16[25,1024]{1,0:T(8,128)(2,1)} %refs_0_.1, bf16[25,256]{1,0:T(8,128)(2,1)} %refs_1_.1, bf16[25,256]{1,0:T(8,128)(2,1)} %refs_2_.1, bf16[47,64]{1,0:T(8,128)(2,1)} %bitcast.7, bf16[47,64]{1,0:T(8,128)(2,1)} %bitcast.8), custom_call_target="tpu_custom_call" | custom-call | flops 2097152 | bytes 262144 | tf_op jit(solution)/shard_map/pack/pallas_call | solution.py:267
  1.6 2.2 %collective-permute-start.31 = (bf16[32,1792]{1,0:T(8,128)(2,1)S(1)}, bf16[32,1792]{1,0:T(8,128)(2,1)S(1)}, u32[]{:S(2)}, u32[]{:S(2)}) collective-permute-start(bf16[32,1792]{1,0:T(8,128)(2,1)S(1)} %pack.1.after_ref.p0_ref), channel_id=1, source_target_pairs={{0,1},{1,2},{2,3},{3,0},{4,5},{5,6},{6,7},{7,4},{8,9},{9,10},{10,1... | collective-permute-start | bytes 344072 | tf_op jit(solution)/shard_map/ppermute | solution.py:29
  3.8 1.5 %collective-permute-start.30 = (bf16[32,1792]{1,0:T(8,128)(2,1)S(1)}, bf16[32,1792]{1,0:T(8,128)(2,1)S(1)}, u32[]{:S(2)}, u32[]{:S(2)}) collective-permute-start(bf16[32,1792]{1,0:T(8,128)(2,1)S(1)} %pack.1.after_ref.p0_ref), channel_id=1, source_target_pairs={{0,3},{1,0},{2,1},{3,2},{4,7},{5,4},{6,5},{7,6},{8,11},{9,8},{10,9... | collective-permute-start | bytes 344072 | tf_op jit(solution)/shard_map/ppermute | solution.py:29
  5.3 1.6 %collective-permute-start.29 = (bf16[32,1792]{1,0:T(8,128)(2,1)S(1)}, bf16[32,1792]{1,0:T(8,128)(2,1)S(1)}, u32[]{:S(2)}, u32[]{:S(2)}) collective-permute-start(bf16[32,1792]{1,0:T(8,128)(2,1)S(1)} %pack.1.after_ref.p0_ref), channel_id=1, source_target_pairs={{0,2},{1,3},{2,0},{3,1},{4,6},{5,7},{6,4},{7,5},{8,10},{9,11},{10,... | collective-permute-start | bytes 344072 | tf_op jit(solution)/shard_map/ppermute | solution.py:29
  6.9 4.0 %load.1 = (bf16[1024,1024]{1,0:T(8,128)(2,1)S(1)}, s32[2,32,1024]{2,1,0:T(8,128)S(1)}, s32[1]{0:T(128)}) custom-call(s32[1024,1024]{1,0:T(8,128)} %e1_ref.1, s32[4096,1024]{1,0:T(8,128)} %e2_ref.1, s32[1,4]{1,0:T(1,128)} %need_ref.1, s32[1,4]{1,0:T(1,128)} %live_ref.1, bf16[32,1792]{1,0:T(8,128)(2,1)S(1)} %pack.1.after_ref.p0_ref), custom_call_target="tpu_custom_call" | custom-call | flops 104857600 | bytes 10485760 | tf_op jit(solution)/shard_map/load/pallas_call | solution.py:289
  11.5 0.0 collective-permute-done.31.p3_ref
  11.5 0.0 collective-permute-done.30.p1_ref
  11.6 0.2 collective-permute-done.29.p2_ref
  11.7 0.8 %first.1 = (f32[48,1024]{1,0:T(8,128)S(1)}, bf16[48,1024]{1,0:T(8,128)(2,1)S(1)}, bf16[48,1024]{1,0:T(8,128)(2,1)S(1)}, bf16[48,1024]{1,0:T(8,128)(2,1)S(1)}) custom-call(bf16[32,1792]{1,0:T(8,128)(2,1)S(1)} %pack.1.after_ref.p0_ref, bf16[32,1792]{1,0:T(8,128)(2,1)S(1)} %collective-permute-done.29.p2_ref, ...), custom_call_target="tpu_custom_call" | custom-call | flops 268435456 | bytes 4194304 | tf_op jit(solution)/shard_map/first/pallas_call | solution.py:313
  12.6 2.7 %collective-permute-start.33 = (bf16[48,1024]{1,0:T(8,128)(2,1)S(1)}, bf16[48,1024]{1,0:T(8,128)(2,1)S(1)}, u32[]{:S(2)}, u32[]{:S(2)}) collective-permute-start(bf16[48,1024]{1,0:T(8,128)(2,1)S(1)} %get-tuple-element.511), channel_id=1, source_target_pairs={{0,64},{4,68},{8,72},{12,76},{16,80},{20,84},{24,88},{28,92},{32,9... | collective-permute-start | bytes 294920 | tf_op jit(solution)/shard_map/ppermute | solution.py:29
  15.3 3.3 %collective-permute-start.32 = (bf16[48,1024]{1,0:T(8,128)(2,1)S(1)}, bf16[48,1024]{1,0:T(8,128)(2,1)S(1)}, u32[]{:S(2)}, u32[]{:S(2)}) collective-permute-start(bf16[48,1024]{1,0:T(8,128)(2,1)S(1)} %get-tuple-element.511), channel_id=1, source_target_pairs={{0,4},{4,8},{8,12},{12,16},{16,20},{20,24},{24,28},{28,32},{32,36}... | collective-permute-start | bytes 294920 | tf_op jit(solution)/shard_map/ppermute | solution.py:29
  18.6 0.0 copy-start
  18.6 8.7 %conditional.1 = (bf16[48,1024]{1,0:T(8,128)(2,1)S(1)}, f32[48,1024]{1,0:T(8,128)S(1)}, s32[2,32,1024]{2,1,0:T(8,128)S(1)}) conditional(s32[]{:T(128)} %bitcast.2, (bf16[48,1024]{1,0:T(8,128)(2,1)S(1)}, bf16[48,1024]{1,0:T(8,128)(2,1)S(1)}, f32[48,1024]{1,0:T(8,128)S(1)}, s32[4096,1024]{1,0:T(8,128)}, ...), branch_computations={%region_0.0_spmd, %region_1.0_spmd, %region_2.0_spmd, %region_3.0_... | conditional | flops 104857600 | bytes 8781888 | solution.py:370
  18.6 3.9 %collective-permute-start.3 = (bf16[48,1024]{1,0:T(8,128)(2,1)S(1)}, bf16[48,1024]{1,0:T(8,128)(2,1)S(1)}, u32[]{:S(2)}, u32[]{:S(2)}) collective-permute-start(bf16[48,1024]{1,0:T(8,128)(2,1)S(1)} %get-tuple-element.311), channel_id=1, source_target_pairs={{0,112},{4,116},{8,120},{12,124},{16,0},{20,4},{24,8},{28,12},{32,... | collective-permute-start | bytes 294920 | tf_op jit(solution)/shard_map/cond/branch_3_fun/ppermute | solution.py:29
  22.4 4.5 %stream.32 = (f32[48,1024]{1,0:T(8,128)S(1)}, s32[2,32,1024]{2,1,0:T(8,128)S(1)}) custom-call(bf16[48,1024]{1,0:T(8,128)(2,1)S(1)} %get-tuple-element.312.z_ref, f32[48,1024]{1,0:T(8,128)S(1)} %get-tuple-element.313.self_ref, s32[4096,1024]{1,0:T(8,128)} %get-tuple-element.314.e2_ref, s32[1,4]{1,0:T(1,128)} %get-tuple-element.315.live_ref), custom_call_target="tpu_custom_call" | custom-call | flops 104857600 | bytes 8388608 | tf_op jit(solution)/shard_map/cond/branch_3_fun/stream/pallas_call | solution.py:340
  27.0 0.0 collective-permute-done.3.in_ref
  27.2 0.0 collective-permute-done.33.z1_ref
  27.2 0.0 collective-permute-done.32.z2_ref
  27.2 0.0 copy-done
  27.3 1.6 %second.1 = (f32[1,1024]{1,0:T(1,128)S(1)}, f32[32,1,128]{2,1,0:T(1,128)S(1)}) custom-call(bf16[48,1024]{1,0:T(8,128)(2,1)S(1)} %collective-permute-done.32.z2_ref, bf16[48,1024]{1,0:T(8,128)(2,1)S(1)} %collective-permute-done.33.z1_ref, bf16[48,1024]{1,0:T(8,128)(2,1)S(1)} %get-tuple-element.515.z3_ref, f32[48,1024]{1,0:T(8,128)S(1)} %get-tuple-element.516.total_ref, ...), custom_call_target="tpu_custom_call" | custom-call | flops 402653184 | bytes 2097152 | tf_op jit(solution)/shard_map/second/pallas_call | solution.py:380
  28.8 12.0 %all_to_all.5.parts_ref = f32[32,1,128]{2,1,0:T(1,128)S(1)} all-to-all(f32[32,1,128]{2,1,0:T(1,128)S(1)} %get-tuple-element.520), channel_id=1, replica_groups=mesh['node'=32,'feat'=4] {'node'}, dimensions={0} | all-to-all | bytes 32768 | tf_op jit(solution)/shard_map/all_to_all | solution.py:398
  40.9 0.7 %final.1 = (f32[1,1024]{1,0:T(1,128)}, f32[1,1]{1,0:T(1,128)}) custom-call(f32[1,1024]{1,0:T(1,128)S(1)} %get-tuple-element.519.loss_ref, f32[32,1,128]{2,1,0:T(1,128)S(1)} %all_to_all.5.parts_ref), custom_call_target="tpu_custom_call" | custom-call | tf_op jit(solution)/shard_map/final/pallas_call | solution.py:399
  (1 shorter events, 0.0 us)
Async XLA Ops:
  1.6 9.9 %collective-permute-start.31 = (bf16[32,1792]{1,0:T(8,128)(2,1)S(1)}, bf16[32,1792]{1,0:T(8,128)(2,1)S(1)}, u32[]{:S(2)}, u32[]{:S(2)}) collective-permute-start(bf16[32,1792]{1,0:T(8,128)(2,1)S(1)} %pack.1.after_ref.p0_ref), channel_id=1, source_target_pairs={{0,1},{1,2},{2,3},{3,0},{4,5},{5,6},{6,7},{7,4},{8,9},{9,10},{10,1... | collective-permute-start | bytes 344072 | tf_op jit(solution)/shard_map/ppermute | solution.py:29
  3.8 7.7 %collective-permute-start.30 = (bf16[32,1792]{1,0:T(8,128)(2,1)S(1)}, bf16[32,1792]{1,0:T(8,128)(2,1)S(1)}, u32[]{:S(2)}, u32[]{:S(2)}) collective-permute-start(bf16[32,1792]{1,0:T(8,128)(2,1)S(1)} %pack.1.after_ref.p0_ref), channel_id=1, source_target_pairs={{0,3},{1,0},{2,1},{3,2},{4,7},{5,4},{6,5},{7,6},{8,11},{9,8},{10,9... | collective-permute-start | bytes 344072 | tf_op jit(solution)/shard_map/ppermute | solution.py:29
  5.3 6.4 %collective-permute-start.29 = (bf16[32,1792]{1,0:T(8,128)(2,1)S(1)}, bf16[32,1792]{1,0:T(8,128)(2,1)S(1)}, u32[]{:S(2)}, u32[]{:S(2)}) collective-permute-start(bf16[32,1792]{1,0:T(8,128)(2,1)S(1)} %pack.1.after_ref.p0_ref), channel_id=1, source_target_pairs={{0,2},{1,3},{2,0},{3,1},{4,6},{5,7},{6,4},{7,5},{8,10},{9,11},{10,... | collective-permute-start | bytes 344072 | tf_op jit(solution)/shard_map/ppermute | solution.py:29
  12.6 14.6 %collective-permute-start.33 = (bf16[48,1024]{1,0:T(8,128)(2,1)S(1)}, bf16[48,1024]{1,0:T(8,128)(2,1)S(1)}, u32[]{:S(2)}, u32[]{:S(2)}) collective-permute-start(bf16[48,1024]{1,0:T(8,128)(2,1)S(1)} %get-tuple-element.511), channel_id=1, source_target_pairs={{0,64},{4,68},{8,72},{12,76},{16,80},{20,84},{24,88},{28,92},{32,9... | collective-permute-start | bytes 294920 | tf_op jit(solution)/shard_map/ppermute | solution.py:29
  15.3 11.9 %collective-permute-start.32 = (bf16[48,1024]{1,0:T(8,128)(2,1)S(1)}, bf16[48,1024]{1,0:T(8,128)(2,1)S(1)}, u32[]{:S(2)}, u32[]{:S(2)}) collective-permute-start(bf16[48,1024]{1,0:T(8,128)(2,1)S(1)} %get-tuple-element.511), channel_id=1, source_target_pairs={{0,4},{4,8},{8,12},{12,16},{16,20},{20,24},{24,28},{28,32},{32,36}... | collective-permute-start | bytes 294920 | tf_op jit(solution)/shard_map/ppermute | solution.py:29
  18.6 8.7 %copy-start = (s32[1024]{0:T(1024)S(1)}, s32[1024]{0:T(1024)}, u32[]{:S(2)}) copy-start(s32[1024]{0:T(1024)} %param.48) | copy-start | bytes 12292
  18.6 8.4 %collective-permute-start.3 = (bf16[48,1024]{1,0:T(8,128)(2,1)S(1)}, bf16[48,1024]{1,0:T(8,128)(2,1)S(1)}, u32[]{:S(2)}, u32[]{:S(2)}) collective-permute-start(bf16[48,1024]{1,0:T(8,128)(2,1)S(1)} %get-tuple-element.311), channel_id=1, source_target_pairs={{0,112},{4,116},{8,120},{12,124},{16,0},{20,4},{24,8},{28,12},{32,... | collective-permute-start | bytes 294920 | tf_op jit(solution)/shard_map/cond/branch_3_fun/ppermute | solution.py:29
